TPU v7x, 256 devices: a whole 4x4x8 slice. The times are simulated.
256 devices in a mesh: ccd: 128 (over z, x, y), row: 2 (over core).
Axes of the slice: x: 4, y: 4, z: 8, core: 2. Of those that a mesh axis runs over, the one named last changes fastest.
Arguments:
- exposure: float32 [128, 48, 2048], P('ccd', 'row'), may hold values from -6 to 6
- row_shift: int32 [128], P('ccd'), may hold values from 0 to 7
- row_fraction: bfloat16 [128, 48], P('ccd', 'row'), may hold values from 0 to 1
- column_shift: int32 [128], P('ccd'), may hold values from 0 to 127
- column_fraction: bfloat16 [128, 2048], P('ccd'), may hold values from 0 to 1
- piece_width: int32 [128, 16], P('ccd'), may hold values from 1 to 128
- route_tile: int32 [128, 16], P('ccd'), may hold values from 0 to 127, as said below
- route_cell: int32 [128, 16], P('ccd'), may hold values from 0 to 31, as said below
- template: float32 [128, 48, 4096], P('ccd', 'row'), may hold values from -6 to 6
- match_kernel: bfloat16 [128, 41, 41], P('ccd'), may hold values from -0.15625 to 0.15625
- detection_kernel: bfloat16 [128, 15, 15], P('ccd'), may hold values from -0.375 to 0.375
Outputs:
- difference: float32 [128, 48, 4096], P('ccd', 'row')
- significance: float32 [128, 48, 4096], P('ccd', 'row')
- noise_level: float32 [], replicated
Inputs may be any that keep to these rules, and one draw needn't show every extreme that they name: Piece p of CCD c lands on tile route_tile[c, p]. Every tile receives at least one piece and at most 32 pieces in all; a quarter of the tiles receive exactly 32. No CCD puts more than 2 pieces on one tile, and some CCDs put exactly 2. `route_cell`: pieces that land on one tile fill different cells.
All inputs are finite; a program needn't handle non-finite values.
Results may differ from a plain program's by a relative error of at most 0.0044.
Values may be sent and summed in bfloat16 or wider, within the bound.
A program may use at most 128 MiB of HBM per device.

v0:
```python
import functools

import jax
import jax.numpy as jnp
from jax import lax
from jax.sharding import Mesh
from jax.sharding import PartitionSpec as P

PW = 128
PAIR = 2
HALO = 8
KS = 41
DK = 15
CCD_ROW = ("ccd_0", "ccd_1", "ccd_2", "row")
CCD = ("ccd_0", "ccd_1", "ccd_2")


stack_depth = 5


def extended_2(x, sides, width):
    for axis, dim in sides:
        size, length = (lax.axis_size(axis), x.shape[dim])
        up = [(i, (i + 1) % size) for i in range(size - 1)]
        down = [(j, i) for i, j in up]
        last = lax.slice_in_dim(x, length - width, length, axis=dim)
        first = lax.slice_in_dim(x, 0, width, axis=dim)
        before = lax.ppermute(last, axis, up)
        after = lax.ppermute(first, axis, down)
        x = jnp.concatenate([before, x, after], axis=dim)
    return x


def one_axis_at_a_time(x, axes):
    return functools.reduce(lax.psum, axes, x)


def passed_along(block, axis, distance):
    devices = range(lax.axis_size(axis))
    route = [(i - distance, i) for i in devices if i - distance in devices]
    return lax.ppermute(block, axis, route)


def warp_columns(padded, column_offset, fraction):
    length = fraction.shape[-1]
    leftward = lax.dynamic_slice_in_dim(padded, column_offset, length, 1).astype(jnp.float32)
    rightward = lax.dynamic_slice_in_dim(padded, column_offset + 1, length, 1).astype(jnp.float32)
    weight = fraction.astype(jnp.float32)[None, :]
    return (1.0 - weight) * leftward + weight * rightward


def band_matrix(kernel):
    extent = kernel.shape[0]
    spread = jnp.arange(2 * PW, dtype=jnp.int32)[:, None] - jnp.arange(PW, dtype=jnp.int32)[None, :]
    picker = (spread[:, :, None] == jnp.arange(extent, dtype=jnp.int32)[None, None, :]).astype(
        jnp.bfloat16
    )
    return jnp.einsum("yd,kjd->ykj", kernel, picker, preferred_element_type=jnp.float32).astype(
        jnp.bfloat16
    )


def banded_filter(source, kernel, height):
    extent = kernel.shape[0]
    margin = extent // 2
    blocks_wide = source.shape[1] // PW
    widened = jnp.pad(source, ((0, 0), (margin, 2 * PW - margin)))
    blocked = widened.reshape(widened.shape[0], blocks_wide + 2, PW)
    windows = jnp.concatenate([blocked[:, :blocks_wide], blocked[:, 1 : blocks_wide + 1]], axis=2)
    banded = band_matrix(kernel)
    running = jnp.zeros((height, blocks_wide, PW), jnp.float32)
    for offset in range(0, extent, stack_depth):
        finish = min(offset + stack_depth, extent)
        stacked = jnp.stack(
            [windows[depth_row : depth_row + height] for depth_row in range(offset, finish)], axis=2
        )
        running = running + jnp.einsum(
            "rcgk,gkj->rcj", stacked, banded[offset:finish], preferred_element_type=jnp.float32
        )
    return running.reshape(height, blocks_wide * PW)


def match_template(template, match_kernel, height):
    rounded = template[0].astype(jnp.bfloat16)
    haloed = extended_2(rounded, (("row", 0),), KS // 2)
    return banded_filter(haloed, match_kernel[0], height)


def detection_pass(difference, detection_kernel, height):
    rounded = difference.astype(jnp.bfloat16)
    haloed = extended_2(rounded, (("row", 0),), DK // 2)
    return banded_filter(haloed, detection_kernel[0], height)


def noise_totals(square_sum, live_count):
    return (one_axis_at_a_time(square_sum, CCD_ROW), one_axis_at_a_time(live_count, CCD_ROW))


def deliver_pieces(
    exposure,
    row_shift,
    row_fraction,
    column_shift,
    column_fraction,
    piece_width,
    route_tile,
    route_cell,
    cell_count,
):
    exposure_band = exposure[0]
    height = exposure_band.shape[0]
    columns = exposure_band.shape[1]
    pieces = columns // PW
    capacity = lax.axis_size(CCD) * PAIR
    below_rows = passed_along(exposure_band[:HALO], "row", -1)
    extended = jnp.concatenate([exposure_band, below_rows], axis=0)
    weight = row_fraction[0].astype(jnp.float32)[:, None]
    upper_rows = lax.dynamic_slice_in_dim(extended, row_shift[0], height, 0)
    lower_rows = lax.dynamic_slice_in_dim(extended, row_shift[0] + 1, height, 0)
    warped_rows = ((1.0 - weight) * upper_rows + weight * lower_rows).astype(jnp.bfloat16)
    padded = jnp.pad(warped_rows, ((0, 0), (0, PW)))
    piece_tile = route_tile[0]
    piece_cell = route_cell[0]
    widths = piece_width[0]
    order_index = jnp.arange(pieces, dtype=jnp.int32)
    earlier = (piece_tile[:, None] == piece_tile[None, :]) & (
        order_index[None, :] < order_index[:, None]
    )
    piece_rank = jnp.sum(earlier.astype(jnp.int32), axis=1)
    target = piece_tile * PAIR + piece_rank
    chooser = jnp.arange(capacity, dtype=jnp.int32)[:, None] == target[None, :]
    chooser_half = chooser.astype(jnp.bfloat16)
    sent_cell = jnp.sum(jnp.where(chooser, piece_cell[None, :] + 1, 0), axis=1) - 1
    sent_width = jnp.sum(jnp.where(chooser, widths[None, :], 0), axis=1)
    lane_index = jnp.arange(PW, dtype=jnp.int32)
    warped = warp_columns(padded, column_shift[0], column_fraction[0]).astype(jnp.bfloat16)
    keep_mask = (lane_index[None, :] < widths[:, None]).reshape(columns)
    warped = jnp.where(keep_mask[None, :], warped, jnp.zeros((), jnp.bfloat16))
    outgoing = jnp.einsum(
        "sp,rpj->srj",
        chooser_half,
        warped.reshape(height, pieces, PW),
        preferred_element_type=jnp.float32,
    ).astype(jnp.bfloat16)
    incoming, got_cell, got_width = (
        lax.all_to_all(outgoing, CCD, split_axis=0, concat_axis=0, tiled=True),
        lax.all_to_all(sent_cell, CCD, split_axis=0, concat_axis=0, tiled=True),
        lax.all_to_all(sent_width, CCD, split_axis=0, concat_axis=0, tiled=True),
    )
    placer = jnp.arange(cell_count, dtype=jnp.int32)[:, None] == got_cell[None, :]
    science = jnp.einsum(
        "qs,srj->rqj", placer.astype(jnp.bfloat16), incoming, preferred_element_type=jnp.float32
    ).reshape(height, cell_count * PW)
    cell_width = jnp.sum(jnp.where(placer, got_width[None, :], 0), axis=1).astype(jnp.int32)
    live_mask = (lane_index[None, :] < cell_width[:, None]).reshape(cell_count * PW)
    return (science, live_mask, cell_width)


def on_device(
    exposure,
    row_shift,
    row_fraction,
    column_shift,
    column_fraction,
    piece_width,
    route_tile,
    route_cell,
    template,
    match_kernel,
    detection_kernel,
):
    height = exposure.shape[1]
    cell_count = template.shape[2] // PW
    science, live_mask, cell_width = deliver_pieces(
        exposure,
        row_shift,
        row_fraction,
        column_shift,
        column_fraction,
        piece_width,
        route_tile,
        route_cell,
        cell_count,
    )
    matched = match_template(template, match_kernel, height)
    difference = jnp.where(live_mask[None, :], science - matched, jnp.zeros((), jnp.float32))
    square_sum = jnp.sum(difference * difference)
    live_count = (height * jnp.sum(cell_width)).astype(jnp.float32)
    filtered = detection_pass(difference, detection_kernel, height)
    total_square, total_count = noise_totals(square_sum, live_count)
    noise_level = total_square / total_count
    detect_weights = detection_kernel[0].astype(jnp.float32)
    kernel_norm = jnp.sum(detect_weights * detect_weights)
    significance = filtered / jnp.sqrt(1.0 + noise_level * kernel_norm)
    return (difference[None], significance[None], noise_level)


def solution(mesh):
    finer = Mesh(
        mesh.devices.reshape(8, 4, 4, mesh.shape["row"]), ("ccd_0", "ccd_1", "ccd_2", "row")
    )
    placed = (
        P(CCD, "row", None),
        P(CCD),
        P(CCD, "row"),
        P(CCD),
        P(CCD, None),
        P(CCD, None),
        P(CCD, None),
        P(CCD, None),
        P(CCD, "row", None),
        P(CCD, None, None),
        P(CCD, None, None),
    )
    return jax.shard_map(
        on_device,
        mesh=finer,
        in_specs=placed,
        out_specs=(P(CCD, "row", None), P(CCD, "row", None), P()),
        check_vma=False,
    )
```

profile of v0, /device:TPU:1, one launch (start us, length us, event | category | flops | bytes accessed | tf_op | source)
XLA Modules:
  0.0 178.2 jit_solution(6839083160252269727)
XLA Ops:
  3.8 6.4 %collective-permute-start.2 = (bf16[20,4096]{1,0:T(8,128)(2,1)}, bf16[20,4096]{1,0:T(8,128)(2,1)}, u32[]{:S(2)}, u32[]{:S(2)}) collective-permute-start(bf16[20,4096]{1,0:T(8,128)(2,1)} %get-tuple-element.60), channel_id=1, source_target_pairs={{1,0},{3,2},{5,4},{7,6},{9,8},{11,10},{13,12},{15,14},{17,16},{19,... | collective-permute-start | bytes 491528 | tf_op jit(solution)/shard_map/ppermute | solution.py:29
  10.3 1.5 slice_bitcast_fusion.11
  11.7 1.9 %collective-permute-start = (f32[8,2048]{1,0:T(8,128)}, f32[8,2048]{1,0:T(8,128)}, u32[]{:S(2)}, u32[]{:S(2)}) collective-permute-start(f32[8,2048]{1,0:T(8,128)} %slice_bitcast_fusion.11), channel_id=1, source_target_pairs={{1,0},{3,2},{5,4},{7,6},{9,8},{11,10},{13,12},{15,14},{17,16},{19,... | collective-permute-start | bytes 196616 | tf_op jit(solution)/shard_map/ppermute | solution.py:41
  15.8 1.3 select_reduce_fusion.2
  17.9 14.8 %all-to-all-start = ((s32[128,2,1]{1,2,0:T(1,128)}), s32[128,2,1]{1,2,0:T(1,128)}, u32[]{:S(2)}, u32[]{:S(2)}) async-start(s32[128,2,1]{1,2,0:T(1,128)} %bitcast.4), calls=%async_computation | async-start | bytes 131072 | tf_op jit(solution)/shard_map/all_to_all | solution.py:147
  33.4 1.6 convert_bitcast_fusion
  35.0 2.5 %fusion.237 = (bf16[5,256,128]{2,0,1:T(8,128)(2,1)}, bf16[5,256,128,1]{2,0,1,3:T(8,128)(2,1)}, bf16[5,256,128,1]{2,0,1,3:T(8,128)(2,1)}, bf16[5,256,128,1]{2,0,1...) fusion(bf16[41,256,128]{2,0,1:T(8,128)(2,1)S(1)} %convert_bitca, ...), kind=kLoop, calls=%fused_computation.399 | loop fusion | bytes 5242880 | tf_op jit(solution)/shard_map/slice | solution.py:78
  39.4 1.3 fusion.238
  41.2 1.4 all_to_all.14
  43.4 12.8 %all-to-all-start.1 = ((s32[128,2,1]{1,2,0:T(1,128)}), s32[128,2,1]{1,2,0:T(1,128)}, u32[]{:S(2)}, u32[]{:S(2)}) async-start(s32[128,2,1]{1,2,0:T(1,128)} %bitcast.401), calls=%async_computation.1 | async-start | bytes 131072 | tf_op jit(solution)/shard_map/all_to_all | solution.py:148
  60.1 1.7 reduce.8
  61.9 4.9 %all-to-all-done.1 = s32[128,2,1]{1,2,0:T(1,128)} async-done(((s32[128,2,1]{1,2,0:T(1,128)}), s32[128,2,1]{1,2,0:T(1,128)}, u32[]{:S(2)}, u32[]{:S(2)}) %all-to-all-start.1) | async-done | bytes 1056 | tf_op jit(solution)/shard_map/all_to_all | solution.py:148
  66.8 1.7 reduce.9
  72.0 1.3 convolution_convert_fusion
  73.3 2.2 %copy.95 = bf16[256,24,128]{2,1,0:T(8,128)(2,1)} copy(bf16[256,24,128]{2,0,1:T(8,128)(2,1)S(1)} %convolution_convert_fusion) | data formatting | bytes 3145728 | tf_op jit(solution)/shard_map/convert_element_type | solution.py:144
  75.5 8.2 %all-to-all-start.2 = ((bf16[256,24,128]{2,1,0:T(8,128)(2,1)}), bf16[256,24,128]{2,1,0:T(8,128)(2,1)S(1)}, u32[]{:S(2)}, u32[]{:S(2)}) async-start(bf16[256,24,128]{2,1,0:T(8,128)(2,1)} %copy.95), calls=%async_computation.2 | async-start | bytes 3145728 | tf_op jit(solution)/shard_map/all_to_all | solution.py:146
  83.7 1.3 fusion.30
  95.6 29.4 %all-to-all-done.2 = bf16[256,24,128]{2,1,0:T(8,128)(2,1)S(1)} async-done(((bf16[256,24,128]{2,1,0:T(8,128)(2,1)}), bf16[256,24,128]{2,1,0:T(8,128)(2,1)S(1)}, u32[]{:S(2)}, u32[]{:S(2)}) %all-to-all-start.2) | async-done | bytes 1572896 | tf_op jit(solution)/shard_map/all_to_all | solution.py:146
  126.3 1.3 collective-permute-start.3
  127.6 3.0 %collective-permute-start.4 = (bf16[7,4096]{1,0:T(8,128)(2,1)S(1)}, bf16[7,4096]{1,0:T(8,128)(2,1)S(1)}, u32[]{:S(2)}, u32[]{:S(2)}) collective-permute-start(bf16[7,4096]{1,0:T(8,128)(2,1)S(1)} %get-tuple-element.58), channel_id=1, source_target_pairs={{1,0},{3,2},{5,4},{7,6},{9,8},{11,10},{13,12},{15,14},{17,16},{19,... | collective-permute-start | bytes 172040 | tf_op jit(solution)/shard_map/ppermute | solution.py:29
  131.4 12.8 %all-reduce.3 = (f32[]{:T(128)}, f32[]{:T(128)}) all-reduce(f32[]{:T(128)} %get-tuple-element.63, f32[]{:T(128)S(6)} %convert_element_type.89), channel_id=1, replica_groups=mesh['ccd_0'=8,'ccd_1'=4,'ccd_2'=4,'row'=2] {'ccd_0'}, use_global_device_ids=true, to_apply=%region_5.6 | all-reduce | flops 2 | bytes 16 | tf_op jit(solution)/shard_map/psum | solution.py:35
  144.2 7.8 %all-reduce.5 = (f32[]{:T(128)}, f32[]{:T(128)}) all-reduce(f32[]{:T(128)} %get-tuple-element.7, f32[]{:T(128)} %get-tuple-element.8), channel_id=1, replica_groups=mesh['ccd_0'=8,'ccd_1'=4,'ccd_2'=4,'row'=2] {'ccd_1'}, use_global_device_ids=true, to_apply=%region_6.7 | all-reduce | flops 2 | bytes 16 | tf_op jit(solution)/shard_map/psum | solution.py:35
  151.9 7.8 %all-reduce.4 = (f32[]{:T(128)}, f32[]{:T(128)}) all-reduce(f32[]{:T(128)} %get-tuple-element.11, f32[]{:T(128)} %get-tuple-element.12), channel_id=1, replica_groups=mesh['ccd_0'=8,'ccd_1'=4,'ccd_2'=4,'row'=2] {'ccd_2'}, use_global_device_ids=true, to_apply=%region_7.8 | all-reduce | flops 2 | bytes 16 | tf_op jit(solution)/shard_map/psum | solution.py:35
  159.8 9.8 %all-reduce.6 = (f32[]{:T(128)}, f32[]{:T(128)}) all-reduce(f32[]{:T(128)} %get-tuple-element.9, f32[]{:T(128)} %get-tuple-element.10), channel_id=1, replica_groups=mesh['ccd_0'=8,'ccd_1'=4,'ccd_2'=4,'row'=2] {'row'}, use_global_device_ids=true, to_apply=%region_8.9 | all-reduce | flops 2 | bytes 16 | tf_op jit(solution)/shard_map/psum | solution.py:35
  (128 shorter events, 33.1 us)
Async XLA Ops:
  0.6 32.8 %copy-start = (bf16[1,41,41]{2,1,0:T(8,128)(2,1)S(1)}, bf16[1,41,41]{2,1,0:T(8,128)(2,1)}, u32[]{:S(2)}) copy-start(bf16[1,41,41]{2,1,0:T(8,128)(2,1)} %param.20) | copy-start | bytes 10090
  0.6 32.0 %copy-start.1 = (f32[1,24,4096]{2,1,0:T(8,128)S(1)}, f32[1,24,4096]{2,1,0:T(8,128)}, u32[]{:S(2)}) copy-start(f32[1,24,4096]{2,1,0:T(8,128)} %param.19) | copy-start | bytes 1179652
  0.7 32.1 %copy-start.18 = (s32[1,16]{1,0:T(1,128)S(1)}, s32[1,16]{1,0:T(1,128)}, u32[]{:S(2)}) copy-start(s32[1,16]{1,0:T(1,128)} %param.16) | copy-start | bytes 196
  2.5 81.2 %collective-permute-start.1 = (bf16[20,4096]{1,0:T(8,128)(2,1)}, bf16[20,4096]{1,0:T(8,128)(2,1)}, u32[]{:S(2)}, u32[]{:S(2)}) collective-permute-start(bf16[20,4096]{1,0:T(8,128)(2,1)} %get-tuple-element.59), channel_id=1, source_target_pairs={{0,1},{2,3},{4,5},{6,7},{8,9},{10,11},{12,13},{14,15},{16,17},{18,... | collective-permute-start | bytes 491528 | tf_op jit(solution)/shard_map/ppermute | solution.py:28
  3.8 79.9 %collective-permute-start.2 = (bf16[20,4096]{1,0:T(8,128)(2,1)}, bf16[20,4096]{1,0:T(8,128)(2,1)}, u32[]{:S(2)}, u32[]{:S(2)}) collective-permute-start(bf16[20,4096]{1,0:T(8,128)(2,1)} %get-tuple-element.60), channel_id=1, source_target_pairs={{1,0},{3,2},{5,4},{7,6},{9,8},{11,10},{13,12},{15,14},{17,16},{19,... | collective-permute-start | bytes 491528 | tf_op jit(solution)/shard_map/ppermute | solution.py:29
  11.7 58.3 %collective-permute-start = (f32[8,2048]{1,0:T(8,128)}, f32[8,2048]{1,0:T(8,128)}, u32[]{:S(2)}, u32[]{:S(2)}) collective-permute-start(f32[8,2048]{1,0:T(8,128)} %slice_bitcast_fusion.11), channel_id=1, source_target_pairs={{1,0},{3,2},{5,4},{7,6},{9,8},{11,10},{13,12},{15,14},{17,16},{19,... | collective-permute-start | bytes 196616 | tf_op jit(solution)/shard_map/ppermute | solution.py:41
  17.9 25.6 %all-to-all-start = ((s32[128,2,1]{1,2,0:T(1,128)}), s32[128,2,1]{1,2,0:T(1,128)}, u32[]{:S(2)}, u32[]{:S(2)}) async-start(s32[128,2,1]{1,2,0:T(1,128)} %bitcast.4), calls=%async_computation | async-start | bytes 131072 | tf_op jit(solution)/shard_map/all_to_all | solution.py:147
  35.0 2.6 %copy-start.19 = (bf16[1,24]{1,0:T(2,128)(2,1)S(1)}, bf16[1,24]{1,0:T(2,128)(2,1)}, u32[]{:S(2)}) copy-start(bf16[1,24]{1,0:T(2,128)(2,1)} %param.13) | copy-start | bytes 148
  35.0 3.1 %copy-start.15 = (bf16[1,2048]{1,0:T(2,128)(2,1)S(1)}, bf16[1,2048]{1,0:T(2,128)(2,1)}, u32[]{:S(2)}) copy-start(bf16[1,2048]{1,0:T(2,128)(2,1)} %param.15) | copy-start | bytes 12292
  35.0 3.7 %copy-start.16 = (bf16[1,15,15]{2,1,0:T(8,128)(2,1)S(1)}, bf16[1,15,15]{2,1,0:T(8,128)(2,1)}, u32[]{:S(2)}) copy-start(bf16[1,15,15]{2,1,0:T(8,128)(2,1)} %param.21) | copy-start | bytes 1354
  39.4 30.7 %copy-start.13 = (f32[1,24,2048]{2,1,0:T(8,128)S(1)}, f32[1,24,2048]{2,1,0:T(8,128)}, u32[]{:S(2)}) copy-start(f32[1,24,2048]{2,1,0:T(8,128)} %param.11) | copy-start | bytes 589828
  43.4 23.4 %all-to-all-start.1 = ((s32[128,2,1]{1,2,0:T(1,128)}), s32[128,2,1]{1,2,0:T(1,128)}, u32[]{:S(2)}, u32[]{:S(2)}) async-start(s32[128,2,1]{1,2,0:T(1,128)} %bitcast.401), calls=%async_computation.1 | async-start | bytes 131072 | tf_op jit(solution)/shard_map/all_to_all | solution.py:148
  75.5 49.5 %all-to-all-start.2 = ((bf16[256,24,128]{2,1,0:T(8,128)(2,1)}), bf16[256,24,128]{2,1,0:T(8,128)(2,1)S(1)}, u32[]{:S(2)}, u32[]{:S(2)}) async-start(bf16[256,24,128]{2,1,0:T(8,128)(2,1)} %copy.95), calls=%async_computation.2 | async-start | bytes 3145728 | tf_op jit(solution)/shard_map/all_to_all | solution.py:146
  87.6 1.5 copy-start.8
  89.1 1.0 copy-start.7
  89.8 1.1 copy-start.6
  90.8 1.1 copy-start.5
  91.6 1.1 copy-start.4
  92.6 1.1 copy-start.3
  93.3 1.1 copy-start.2
  126.3 45.2 %collective-permute-start.3 = (bf16[7,4096]{1,0:T(8,128)(2,1)S(1)}, bf16[7,4096]{1,0:T(8,128)(2,1)S(1)}, u32[]{:S(2)}, u32[]{:S(2)}) collective-permute-start(bf16[7,4096]{1,0:T(8,128)(2,1)S(1)} %get-tuple-element.57), channel_id=1, source_target_pairs={{0,1},{2,3},{4,5},{6,7},{8,9},{10,11},{12,13},{14,15},{16,17},{18,... | collective-permute-start | bytes 172040 | tf_op jit(solution)/shard_map/ppermute | solution.py:28
  127.6 43.9 %collective-permute-start.4 = (bf16[7,4096]{1,0:T(8,128)(2,1)S(1)}, bf16[7,4096]{1,0:T(8,128)(2,1)S(1)}, u32[]{:S(2)}, u32[]{:S(2)}) collective-permute-start(bf16[7,4096]{1,0:T(8,128)(2,1)S(1)} %get-tuple-element.58), channel_id=1, source_target_pairs={{1,0},{3,2},{5,4},{7,6},{9,8},{11,10},{13,12},{15,14},{17,16},{19,... | collective-permute-start | bytes 172040 | tf_op jit(solution)/shard_map/ppermute | solution.py:29
  172.8 1.1 copy-start.11
  172.9 1.6 copy-start.10
  (4 other events, 3.6 us)
where the time goes:
time: 179 us; the launch traced here: 178 us
  starting transfers between devices  49.8 us (28%)
  blocking collectives  38.1 us (21%)
  waiting for transfers between devices  35.1 us (20%)
  other arithmetic  18.9 us (11%)
  local copies, waits for them, and re-layouts  17.6 us (10%)
  matrix products  12.2 us (7%)
  between operations  6.42 us (4%)
    psum x4, blocking collectives, one_axis_at_a_time(): return functools.reduce(lax.psum, axes, x)  38.1 us
    all_to_all x1, waiting for transfers between devices, deliver_pieces(): lax.all_to_all(outgoing, CCD, split_axis=0, concat_axis=0, tiled=True)  29.4 us
    all_to_all x1, starting transfers between devices, deliver_pieces(): lax.all_to_all(sent_cell, CCD, split_axis=0, concat_axis=0, tiled=True)  14.8 us
    all_to_all x1, starting transfers between devices, deliver_pieces(): lax.all_to_all(sent_width, CCD, split_axis=0, concat_axis=0, tiled=True)  12.8 us
    ppermute x2, starting transfers between devices, extended_2(): after = lax.ppermute(first, axis, down)  9.48 us
    all_to_all x1, starting transfers between devices, deliver_pieces(): lax.all_to_all(outgoing, CCD, split_axis=0, concat_axis=0, tiled=True)  8.2 us
    dot_general x12, matrix products, banded_filter(): jnp.einsum('rcgk,gkj->rcj', stacked, banded[offset:finish], preferred_ele...  7.72 us
    all_to_all x1, waiting for transfers between devices, deliver_pieces(): lax.all_to_all(sent_width, CCD, split_axis=0, concat_axis=0, tiled=True)  4.92 us
  transfers between devices with their start and end apart: 8, of which 3 were waited for; matrix products, arithmetic and copies ran while one was open for 20% of the time, Pallas kernels for 0%

commit v1 on v0

v1 whole, which is shorter than its diff:
```python
import functools

import jax
import jax.numpy as jnp
from jax import lax
from jax.experimental import pallas as pl
from jax.experimental.pallas import tpu as pltpu
from jax.sharding import Mesh
from jax.sharding import PartitionSpec as P

PW = 128
HALO = 8
KS = 41
DK = 15
NZ, NX, NY = 8, 4, 4
GROUP = NZ * NY
NP = 16
CAP = 32
ROWS = 24
FR = ROWS // NZ
FL = PW // NY
MESH = pl.DeviceIdType.MESH
CCD = ("ccd_0", "ccd_1", "ccd_2")
F32, BF16, I32 = jnp.float32, jnp.bfloat16, jnp.int32


def lanes_of(shape):
    return lax.broadcasted_iota(I32, shape, len(shape) - 1)


def column_of(row, count):
    spread = jnp.broadcast_to(row, (count, count))
    pick = lax.broadcasted_iota(I32, (count, count), 0) == lanes_of((count, count))
    return jnp.sum(jnp.where(pick, spread, 0.0), axis=1, keepdims=True)


def down(x):
    rolled = pltpu.roll(x, 1, 0)
    return jnp.where(lax.broadcasted_iota(I32, x.shape, 0) == 0, 0.0, rolled)


def up(x):
    rolled = pltpu.roll(x, x.shape[0] - 1, 0)
    return jnp.where(lax.broadcasted_iota(I32, x.shape, 0) == x.shape[0] - 1, 0.0, rolled)


def build_bands(kernel_ref, extent, base_lo, base_hi, bands):
    depth = lax.broadcasted_iota(I32, (extent, 2 * PW), 0)
    place = lanes_of((extent, 2 * PW))
    picker = (lax.rem(depth + place, 2 * PW) == 0).astype(F32).astype(BF16)
    turned = jnp.dot(kernel_ref[...], picker, preferred_element_type=F32)
    for s in range(8):
        rolled = pltpu.roll(turned, s, 1) if s else turned
        base_lo[pl.ds(s, extent, stride=8), :] = rolled[:, :PW]
        base_hi[pl.ds(s, extent, stride=8), :] = rolled[:, PW:]
    bands[0:2 * PW, PW:] = jnp.zeros((2 * PW, PW), BF16)
    bands[extent * 2 * PW:(extent + 1) * 2 * PW, :PW] = jnp.zeros((2 * PW, PW), BF16)
    lane = lanes_of((8, PW))

    def step(a, carry):
        lo = base_lo[pl.ds(pl.multiple_of(a * 8, 8), 8), :]
        hi = base_hi[pl.ds(pl.multiple_of(a * 8, 8), 8), :]
        for pair in range(8):
            near, far = [], []
            for m in (2 * pair, 2 * pair + 1):
                shift = 8 * m
                rlo = pltpu.roll(lo, shift, 1) if shift else lo
                rhi = pltpu.roll(hi, shift, 1) if shift else hi
                near.append(jnp.where(lane >= shift, rlo, rhi))
                far.append(jnp.where(lane >= shift, rhi, rlo))
            for value, start in ((near, 16 * pair), (far, PW + 16 * pair)):
                block = jnp.concatenate(value, axis=0).astype(BF16)
                at = pl.multiple_of(a * 2 * PW + start, 16)
                bands[pl.ds(at, 16), 0:PW] = block
                after = pl.multiple_of((a + 1) * 2 * PW + start, 16)
                bands[pl.ds(after, 16), PW:2 * PW] = block
        return carry

    lax.fori_loop(0, extent, step, 0)


def build_windows(rows_ref, count, margin, windows):
    lane = lanes_of((CAP, PW))

    def step(h, carry):
        for parity in range(2):
            shifted = pltpu.roll(rows_ref[2 * h + parity].astype(F32), margin, 1)
            first = jnp.where(lane < margin, down(shifted), shifted)
            second = jnp.where(lane < margin, shifted, up(shifted))
            at = pl.ds(pl.multiple_of(h * CAP, CAP), CAP)
            windows[parity, at, 0:PW] = first.astype(BF16)
            windows[parity, at, PW:2 * PW] = second.astype(BF16)
        return carry

    lax.fori_loop(0, count // 2, step, 0)


def banded(windows, bands, extent, per_step, total):
    half = ROWS // 2 * CAP
    taps = (extent + 1) // 2

    def part(step):
        left = []
        for i in range(per_step):
            at = pl.ds(pl.multiple_of((step * per_step + i) * CAP, CAP), half)
            left += [windows[0, at, :], windows[1, at, :]]
        depth = per_step * 4 * PW
        right = bands[pl.ds(pl.multiple_of(step * depth, depth), depth), :]
        return jnp.dot(jnp.concatenate(left, axis=1), right, preferred_element_type=F32)

    total[...] = part(0)

    def step(i, carry):
        total[...] += part(i)
        return carry

    lax.fori_loop(1, taps // per_step, step, 0)


def kernel(
    exposure, template, row_shift, column_shift, row_fraction, column_fraction,
    piece_width, route_tile, route_cell, match_kernel, detection_kernel,
    difference, significance, noise,
    ext, hx, tf, tb, rfw, cfw, meta, msg, rcv, agb, acc, outg, grcv,
    base_lo, base_hi, bands, dbands, windows, dwindows, total, matched, diffs, db,
    arsrc, arcv, ar2src, arcv2, local, sends, recvs,
):
    z, x, y = (lax.axis_index(a) for a in CCD)
    c = lax.axis_index("row")
    me = z * NY + y

    def zpeer(dz, dy):
        pz = lax.rem(z + dz, NZ)
        py = lax.rem(y + dy, NY)
        return pz, py, {"ccd_0": pz, "ccd_2": py}

    def xpeer(dx, dc=0):
        return {"ccd_1": lax.rem(x + dx, NX), "row": lax.rem(c + dc, 2)}

    partner = {"row": 1 - c}
    near = [(dz, dy) for dz in range(NZ) for dy in range(NY) if dz or dy]
    across = [(dx, dc) for dx in range(NX) for dc in range(2) if dx or dc]

    def send(src, dst, stage, device, slot=None):
        pltpu.make_async_remote_copy(
            src_ref=src, dst_ref=dst, send_sem=sends.at[stage], recv_sem=recvs.at[stage if slot is None else slot],
            device_id=device, device_id_type=MESH,
        ).start()

    def arrived(ref, slot):
        pltpu.make_async_copy(ref, ref, recvs.at[slot]).wait()

    def sent(ref, stage):
        pltpu.make_async_copy(ref, ref, sends.at[stage]).wait()

    for p in range(NP):
        pltpu.make_async_copy(exposure.at[:, pl.ds(p * PW, PW)], ext.at[pl.ds(0, ROWS), p, :], local.at[0]).start()
    for q in range(CAP):
        pltpu.make_async_copy(template.at[:, pl.ds(q * PW, PW)], tf.at[:, q, :], local.at[1]).start()
    barrier = pltpu.get_barrier_semaphore()
    for dz, dy in near:
        pl.semaphore_signal(barrier, inc=1, device_id=zpeer(dz, dy)[2], device_id_type=MESH)
    for dx, dc in across:
        pl.semaphore_signal(barrier, inc=1, device_id=xpeer(dx, dc), device_id_type=MESH)

    fractions = row_fraction[...].astype(F32)
    for r in range(ROWS):
        rfw[r] = jnp.broadcast_to(fractions[:, r:r + 1], (1, PW))
    columns = column_fraction[...].astype(F32)
    for p in range(NP):
        cfw[p:p + 1, :] = columns[:, p * PW:(p + 1) * PW]
    lane16 = lanes_of((NP, PW))
    width16 = column_of(piece_width[...].astype(F32), NP)
    tile16 = column_of(route_tile[...].astype(F32), NP)
    cell16 = column_of(route_cell[...].astype(F32), NP)
    meta[...] = jnp.where(lane16 == 96, tile16, jnp.where(lane16 == 97, cell16, jnp.where(lane16 == 98, width16, 0.0)))
    build_bands(match_kernel, KS, base_lo, base_hi, bands)
    margin = KS // 2
    pltpu.make_async_copy(tf, tf, local.at[1]).wait()

    def round_template(r, carry):
        tb[margin + r] = tf[r].astype(BF16)
        return carry

    lax.fori_loop(0, ROWS, round_template, 0)

    def zero_template(r, carry):
        tb[c * (ROWS + margin) + r] = jnp.zeros((CAP, PW), BF16)
        return carry

    lax.fori_loop(0, margin, zero_template, 0)
    pltpu.make_async_copy(ext.at[pl.ds(0, ROWS)], ext.at[pl.ds(0, ROWS)], local.at[0]).wait()
    pl.semaphore_wait(barrier, len(near) + len(across))

    send(ext.at[pl.ds(0, HALO)], hx, 0, partner)
    send(tb.at[pl.ds(margin + (1 - c) * (ROWS - margin), margin)], tb.at[pl.ds(c * (ROWS + margin), margin)], 1, partner)
    arrived(hx, 0)
    keep = jnp.where(c == 0, 1.0, 0.0)
    for r in range(HALO):
        ext[ROWS + r] = hx[r] * keep

    t = row_shift[0]
    s = column_shift[0]
    left_turn = lax.rem(PW - s, PW)
    right_turn = PW - 1 - s
    weight = cfw[...]
    inside = lane16.astype(F32) < width16
    head = meta[...]

    def fragments(pz):
        rows = []
        for j in range(FR):
            r = pz * FR + j
            w = rfw[r]
            mixed = ((1.0 - w) * ext[r + t] + w * ext[r + t + 1]).astype(BF16).astype(F32)
            leftward = pltpu.roll(mixed, left_turn, 1)
            leftward = jnp.where(lane16 < PW - s, leftward, up(leftward))
            rightward = pltpu.roll(mixed, right_turn, 1)
            rightward = jnp.where(lane16 < PW - 1 - s, rightward, up(rightward))
            warped = (1.0 - weight) * leftward + weight * rightward
            rows.append(jnp.where(inside, warped, 0.0))
        out = []
        for py in range(NY):
            value = head
            for j in range(FR):
                turn = (FL * (j - py)) % PW
                moved = pltpu.roll(rows[j], turn, 1) if turn else rows[j]
                value = jnp.where((lane16 >= FL * j) & (lane16 < FL * (j + 1)), moved, value)
            out.append(value.astype(BF16))
        return out

    def spread(dz, carry):
        pz = lax.rem(z + dz, NZ)
        for py, value in enumerate(fragments(pz)):
            msg[pz * NY + py] = value
        for dy in range(NY):
            _, py, device = zpeer(dz, dy)
            send(msg.at[pz * NY + py], rcv.at[me], 2, device)
        return carry

    lax.fori_loop(1, NZ, spread, 0)
    for py, value in enumerate(fragments(z)):
        msg[z * NY + py] = value
    for dy in range(1, NY):
        _, py, device = zpeer(0, dy)
        send(msg.at[z * NY + py], rcv.at[me], 2, device)
    rcv[me] = msg[me]

    arrived(hx_template(tb, margin, c), 1)
    build_windows(tb, ROWS + 2 * margin, margin, windows)
    banded(windows, bands, KS, 3, total)

    def unpair(q, carry):
        at = pl.ds(pl.multiple_of(q * CAP, CAP), CAP)
        matched[2 * q] = total[at, 0:PW]
        matched[2 * q + 1] = total[at, PW:2 * PW]
        return carry

    lax.fori_loop(0, ROWS // 2, unpair, 0)
    build_bands(detection_kernel, DK, base_lo, base_hi, dbands)
    arrived(rcv.at[pl.ds(0, GROUP - 1)], 2)

    for dx in (1, 3, 2):
        send(rcv, agb.at[dx - 1], 3, xpeer(dx), slot=8 + dx)

    def codes(block):
        picks = (lanes_of((8, PW)) == lax.broadcasted_iota(I32, (8, PW), 0) + 96).astype(F32).astype(BF16)
        rows = lax.dot_general(picks, block, (((1,), (1,)), ((), ())), preferred_element_type=F32)
        tile = rows[0:1, :].astype(I32)
        cell = rows[1:2, :].astype(I32)
        tz, tx, ty = tile // (NX * NY), (tile // NY) % NX, tile % NY
        return jnp.where(tx == x, (tz * NY + ty) * CAP + cell, -1)

    chunk = NY * CAP
    chunk_rows = lax.broadcasted_iota(I32, (chunk, GROUP * NP), 0)

    def chosen(code, block, pz):
        hot = (chunk_rows == code - pz * chunk).astype(F32).astype(BF16)
        return jnp.dot(hot, block, preferred_element_type=F32)

    def flat(ref):
        return ref[...].reshape(GROUP * NP, PW)

    def add_block(block, first):
        code = codes(block)

        def step(pz, carry):
            at = pl.ds(pl.multiple_of(pz * chunk, chunk), chunk)
            value = chosen(code, block, pz)
            acc[at, :] = value if first else acc[at, :] + value
            return carry

        lax.fori_loop(0, NZ, step, 0)

    add_block(flat(rcv), True)
    arrived(agb.at[0], 9)
    add_block(flat(agb.at[0]), False)
    arrived(agb.at[2], 11)
    add_block(flat(agb.at[2]), False)
    arrived(agb.at[1], 10)
    block = flat(agb.at[1])
    code = codes(block)

    def finish(pz):
        at = pl.ds(pl.multiple_of(pz * chunk, chunk), chunk)
        value = (acc[at, :] + chosen(code, block, pz)).astype(BF16)
        for py in range(NY):
            outg[pz * NY + py] = value[py * CAP:(py + 1) * CAP]

    def deliver(dz, carry):
        pz = lax.rem(z + dz, NZ)
        finish(pz)
        for dy in range(NY):
            _, py, device = zpeer(dz, dy)
            send(outg.at[pz * NY + py], grcv.at[me], 4, device)
        return carry

    lax.fori_loop(1, NZ, deliver, 0)
    finish(z)
    for dy in range(1, NY):
        _, py, device = zpeer(0, dy)
        send(outg.at[z * NY + py], grcv.at[me], 4, device)
    grcv[me] = outg[me]
    sent(rcv.at[pl.ds(0, GROUP - 1)], 2)
    sent(agb, 3)
    sent(hx, 0)
    sent(tb.at[pl.ds(0, margin)], 1)

    dmargin = DK // 2

    def zero_difference(r, carry):
        db[c * (ROWS + dmargin) + r] = jnp.zeros((CAP, PW), BF16)
        return carry

    lax.fori_loop(0, dmargin, zero_difference, 0)
    arrived(grcv.at[pl.ds(0, GROUP - 1)], 4)

    lane32 = lanes_of((CAP, PW))
    own = grcv[me].astype(F32)
    width32 = jnp.sum(jnp.where(lane32 == 98, own, 0.0), axis=1, keepdims=True)
    live = lane32.astype(F32) < width32

    def subtract(pz, squares):
        parts = [grcv[pz * NY + py].astype(F32) for py in range(NY)]
        for j in range(FR):
            science = None
            for py in range(NY):
                turn = (FL * (py - j)) % PW
                moved = pltpu.roll(parts[py], turn, 1) if turn else parts[py]
                science = moved if science is None else jnp.where(lane32 >= FL * py, moved, science)
            r = pz * FR + j
            value = jnp.where(live, science - matched[r], 0.0)
            diffs[r] = value
            db[dmargin + r] = value.astype(BF16)
            squares = squares + value * value
        return squares

    squares = lax.fori_loop(0, NZ, subtract, jnp.zeros((CAP, PW), F32))
    square_sum = jnp.sum(jnp.sum(squares, axis=1, keepdims=True), axis=0, keepdims=True)
    live_count = ROWS * jnp.sum(width32, axis=0, keepdims=True)
    lane1 = lanes_of((1, PW))
    arsrc[...] = jnp.where(lane1 == 0, square_sum, jnp.where(lane1 == 1, live_count, 0.0))
    for dz, dy in near:
        send(arsrc, arcv.at[me], 5, zpeer(dz, dy)[2])
    arcv[me] = arsrc[...]
    send(db.at[pl.ds(dmargin + (1 - c) * (ROWS - dmargin), dmargin)], db.at[pl.ds(c * (ROWS + dmargin), dmargin)], 6, partner)
    for q in range(CAP):
        pltpu.make_async_copy(diffs.at[:, q, :], difference.at[:, pl.ds(q * PW, PW)], local.at[2]).start()
    arrived(hx_template(db, dmargin, c), 6)

    build_windows(db, ROWS + 2 * dmargin, dmargin, dwindows)
    banded(dwindows, dbands, DK, 2, total)
    arrived(arcv.at[pl.ds(0, GROUP - 1)], 5)
    ar2src[...] = jnp.sum(arcv[...], axis=0)
    for dx, dc in across:
        send(ar2src, arcv2.at[x * 2 + c], 7, xpeer(dx, dc))
    arcv2[x * 2 + c] = ar2src[...]
    arrived(arcv2.at[pl.ds(0, 7)], 7)
    sums = jnp.sum(arcv2[...], axis=0)
    whole_square = jnp.sum(jnp.where(lane1 == 0, sums, 0.0), axis=1, keepdims=True)
    whole_count = jnp.sum(jnp.where(lane1 == 1, sums, 0.0), axis=1, keepdims=True)
    level = whole_square / whole_count
    taps = detection_kernel[...].astype(F32)
    norm = jnp.sum(jnp.sum(taps * taps, axis=1, keepdims=True), axis=0, keepdims=True)
    scale = jnp.broadcast_to(1.0 / jnp.sqrt(1.0 + level * norm), (CAP, PW))
    noise[...] = jnp.broadcast_to(level, (1, PW))

    def rescale(q, carry):
        at = pl.ds(pl.multiple_of(q * CAP, CAP), CAP)
        tf[2 * q] = total[at, 0:PW] * scale
        tf[2 * q + 1] = total[at, PW:2 * PW] * scale
        return carry

    lax.fori_loop(0, ROWS // 2, rescale, 0)
    for q in range(CAP):
        pltpu.make_async_copy(tf.at[:, q, :], significance.at[:, pl.ds(q * PW, PW)], local.at[3]).start()
    sent(grcv.at[pl.ds(0, GROUP - 1)], 4)
    sent(arcv.at[pl.ds(0, GROUP - 1)], 5)
    sent(db.at[pl.ds(0, dmargin)], 6)
    sent(arcv2.at[pl.ds(0, 7)], 7)
    pltpu.make_async_copy(diffs, diffs, local.at[2]).wait()
    pltpu.make_async_copy(tf, tf, local.at[3]).wait()


def hx_template(ref, margin, c):
    return ref.at[pl.ds((1 - c) * (ROWS + margin), margin)]


def on_device(
    exposure, row_shift, row_fraction, column_shift, column_fraction, piece_width,
    route_tile, route_cell, template, match_kernel, detection_kernel,
):
    vmem = pl.BlockSpec(memory_space=pltpu.VMEM)
    smem = pl.BlockSpec(memory_space=pltpu.SMEM)
    far = pl.BlockSpec(memory_space=pl.ANY)
    wide = template.shape[2]
    margin, dmargin = KS // 2, DK // 2
    difference, significance, noise = pl.pallas_call(
        kernel,
        out_shape=(
            jax.ShapeDtypeStruct((ROWS, wide), F32),
            jax.ShapeDtypeStruct((ROWS, wide), F32),
            jax.ShapeDtypeStruct((1, PW), F32),
        ),
        in_specs=[far, far, smem, smem] + [vmem] * 7,
        out_specs=(far, far, vmem),
        scratch_shapes=[
            pltpu.VMEM((ROWS + HALO, NP, PW), F32),
            pltpu.VMEM((HALO, NP, PW), F32),
            pltpu.VMEM((ROWS, CAP, PW), F32),
            pltpu.VMEM((ROWS + 2 * margin, CAP, PW), BF16),
            pltpu.VMEM((ROWS, 1, PW), F32),
            pltpu.VMEM((NP, PW), F32),
            pltpu.VMEM((NP, PW), F32),
            pltpu.VMEM((GROUP, NP, PW), BF16),
            pltpu.VMEM((GROUP, NP, PW), BF16),
            pltpu.VMEM((NX - 1, GROUP, NP, PW), BF16),
            pltpu.VMEM((GROUP * CAP, PW), F32),
            pltpu.VMEM((GROUP, CAP, PW), BF16),
            pltpu.VMEM((GROUP, CAP, PW), BF16),
            pltpu.VMEM((48 * 8, PW), F32),
            pltpu.VMEM((48 * 8, PW), F32),
            pltpu.VMEM(((KS + 1) * 2 * PW, 2 * PW), BF16),
            pltpu.VMEM(((DK + 1) * 2 * PW, 2 * PW), BF16),
            pltpu.VMEM((2, (ROWS // 2 + margin) * CAP, 2 * PW), BF16),
            pltpu.VMEM((2, (ROWS // 2 + dmargin) * CAP, 2 * PW), BF16),
            pltpu.VMEM((ROWS // 2 * CAP, 2 * PW), F32),
            pltpu.VMEM((ROWS, CAP, PW), F32),
            pltpu.VMEM((ROWS, CAP, PW), F32),
            pltpu.VMEM((ROWS + 2 * dmargin, CAP, PW), BF16),
            pltpu.VMEM((1, PW), F32),
            pltpu.VMEM((GROUP, 1, PW), F32),
            pltpu.VMEM((1, PW), F32),
            pltpu.VMEM((8, 1, PW), F32),
            pltpu.SemaphoreType.DMA((4,)),
            pltpu.SemaphoreType.DMA((8,)),
            pltpu.SemaphoreType.DMA((12,)),
        ],
        compiler_params=pltpu.CompilerParams(collective_id=0, has_side_effects=True, vmem_limit_bytes=60 * 1024 * 1024),
        name="warp_match_detect",
    )(
        exposure[0], template[0], row_shift, column_shift, row_fraction, column_fraction,
        piece_width, route_tile, route_cell, match_kernel[0], detection_kernel[0],
    )
    return difference[None], significance[None], noise[0, 0]


def solution(mesh):
    finer = Mesh(
        mesh.devices.reshape(NZ, NX, NY, mesh.shape["row"]), ("ccd_0", "ccd_1", "ccd_2", "row")
    )
    placed = (
        P(CCD, "row", None),
        P(CCD),
        P(CCD, "row"),
        P(CCD),
        P(CCD, None),
        P(CCD, None),
        P(CCD, None),
        P(CCD, None),
        P(CCD, "row", None),
        P(CCD, None, None),
        P(CCD, None, None),
    )
    return jax.shard_map(
        on_device,
        mesh=finer,
        in_specs=placed,
        out_specs=(P(CCD, "row", None), P(CCD, "row", None), P()),
        check_vma=False,
    )
```

time: 179 us -> 58.8 us (0.33)
  Pallas kernels: 0 us -> 52.9 us
  starting transfers between devices: 49.8 us -> 0 us
  blocking collectives: 38.1 us -> 0 us
  waiting for transfers between devices: 35.1 us -> 0 us
  other arithmetic: 18.9 us -> 0 us
  local copies, waits for them, and re-layouts: 17.6 us -> 2.57 us
  matrix products: 12.2 us -> 0 us
  between operations: 6.42 us -> 3.11 us
    pallas_call x0 -> x1, Pallas kernels: none -> 52.9 us  [on_device(): pl.pallas_call(kernel, out_shape=(jax.ShapeDtypeStruct((ROWS, wide), F32)...]
    psum x4 -> x0, blocking collectives: 38.1 us -> none  [one_axis_at_a_time(): return functools.reduce(lax.psum, axes, x)]
    all_to_all x3 -> x0, starting transfers between devices: 35.8 us -> none  [the longest x1 14.8 us: deliver_pieces(): lax.all_to_all(sent_cell, CCD, split_axis=0, concat_axis=0, tiled=True)]
    all_to_all x3 -> x0, waiting for transfers between devices: 35.1 us -> none  [the longest x1 29.4 us: deliver_pieces(): lax.all_to_all(outgoing, CCD, split_axis=0, concat_axis=0, tiled=True)]
    ppermute x5 -> x0, starting transfers between devices: 14 us -> none  [the longest x2 9.48 us: extended_2(): after = lax.ppermute(first, axis, down)]
    dot_general x16 -> x0, matrix products: 12.2 us -> none  [the longest x12 7.72 us: banded_filter(): jnp.einsum('rcgk,gkj->rcj', stacked, banded[offset:finish], preferred_ele...]
    slice x8 -> x0, local copies, waits for them, and re-layouts: 7.22 us -> none  [the longest x3 4.57 us: banded_filter(): banded[offset:finish]]
    convert_element_type x6 -> x0, other arithmetic: 3.67 us -> none  [the longest x2 1.09 us: match_template(): rounded = template[0].astype(jnp.bfloat16)]
  transfers between devices with their start and end apart: 8 -> 0, of which waited for: 3 -> 0; matrix products, arithmetic and copies ran while one was open for 20% -> 0% of each run, Pallas kernels for 0% -> 0%
where the time goes in v1:
time: 58.8 us; the launch traced here: 58.6 us
  Pallas kernels  52.9 us (90%)
  between operations  3.11 us (5%)
  local copies, waits for them, and re-layouts  2.57 us (4%)
    pallas_call x1, Pallas kernels, on_device(): pl.pallas_call(kernel, out_shape=(jax.ShapeDtypeStruct((ROWS, wide), F32)...  52.9 us
    unnamed x6, local copies, waits for them, and re-layouts  2.57 us

profile of v1, /device:TPU:1, one launch (start us, length us, event | category | flops | bytes accessed | tf_op | source)
XLA Modules:
  0.0 58.6 jit_solution(684400255240812352)
XLA Ops:
  1.9 52.9 %warp_match_detect.1 = (f32[24,4096]{1,0:T(8,128)}, f32[24,4096]{1,0:T(8,128)}, f32[1,128]{1,0:T(1,128)}) custom-call(f32[24,2048]{1,0:T(8,128)} %bitcast.11, f32[24,4096]{1,0:T(8,128)} %bitcast.8, s32[1]{0:T(128)S(6)} %copy.17.row_shift, s32[1]{0:T(128)S(6)} %copy.18.column_shift, bf16[1,24]{1,0:T(2,128)(2,1)} %row_fraction.1, ...), custom_call_target="tpu_custom_call" | custom-call | tf_op jit(solution)/shard_map/warp_match_detect/pallas_call | solution.py:418
  54.9 0.0 copy-start
  54.9 1.8 %copy.19 = f32[1,24,4096]{2,1,0:T(8,128)} copy(f32[1,24,4096]{2,1,0:T(8,128)} %bitcast.10) | data formatting | bytes 786432
  56.7 0.0 copy-done
  56.7 0.0 copy-start.1
  56.7 0.7 %copy.20 = f32[1,24,4096]{2,1,0:T(8,128)} copy(f32[1,24,4096]{2,1,0:T(8,128)S(1)} %bitcast.9) | data formatting | bytes 786432
  57.4 0.0 copy-done.1
Async XLA Ops:
  54.9 1.8 %copy-start = (f32[24,4096]{1,0:T(8,128)S(1)}, f32[24,4096]{1,0:T(8,128)}, u32[]{:S(2)}) copy-start(f32[24,4096]{1,0:T(8,128)} %get-tuple-element.7) | copy-start | bytes 1179652
  56.7 0.8 %copy-start.1 = (f32[1,128]{1,0:T(1,128)S(1)}, f32[1,128]{1,0:T(1,128)}, u32[]{:S(2)}) copy-start(f32[1,128]{1,0:T(1,128)} %get-tuple-element.8) | copy-start | bytes 1540

commit v2 on v1

--- a/solution.py
+++ b/solution.py
@@ -19,6 +19,7 @@
 ROWS = 24
 FR = ROWS // NZ
 FL = PW // NY
+EARLY = 18
 MESH = pl.DeviceIdType.MESH
 CCD = ("ccd_0", "ccd_1", "ccd_2")
 F32, BF16, I32 = jnp.float32, jnp.bfloat16, jnp.int32
@@ -44,7 +45,7 @@
     return jnp.where(lax.broadcasted_iota(I32, x.shape, 0) == x.shape[0] - 1, 0.0, rolled)
 
 
-def build_bands(kernel_ref, extent, base_lo, base_hi, bands):
+def band_bases(kernel_ref, extent, base_lo, base_hi, bands):
     depth = lax.broadcasted_iota(I32, (extent, 2 * PW), 0)
     place = lanes_of((extent, 2 * PW))
     picker = (lax.rem(depth + place, 2 * PW) == 0).astype(F32).astype(BF16)
@@ -55,6 +56,9 @@
         base_hi[pl.ds(s, extent, stride=8), :] = rolled[:, PW:]
     bands[0:2 * PW, PW:] = jnp.zeros((2 * PW, PW), BF16)
     bands[extent * 2 * PW:(extent + 1) * 2 * PW, :PW] = jnp.zeros((2 * PW, PW), BF16)
+
+
+def build_bands(base_lo, base_hi, bands, first, last):
     lane = lanes_of((8, PW))
 
     def step(a, carry):
@@ -76,28 +80,47 @@
                 bands[pl.ds(after, 16), PW:2 * PW] = block
         return carry
 
-    lax.fori_loop(0, extent, step, 0)
-
-
-def build_windows(rows_ref, count, margin, windows):
+    lax.fori_loop(first, last, step, 0)
+
+
+def build_windows(rows_ref, start, count, margin, windows, unroll):
     lane = lanes_of((CAP, PW))
 
-    def step(h, carry):
-        for parity in range(2):
-            shifted = pltpu.roll(rows_ref[2 * h + parity].astype(F32), margin, 1)
-            first = jnp.where(lane < margin, down(shifted), shifted)
-            second = jnp.where(lane < margin, shifted, up(shifted))
-            at = pl.ds(pl.multiple_of(h * CAP, CAP), CAP)
-            windows[parity, at, 0:PW] = first.astype(BF16)
-            windows[parity, at, PW:2 * PW] = second.astype(BF16)
-        return carry
-
-    lax.fori_loop(0, count // 2, step, 0)
-
-
-def banded(windows, bands, extent, per_step, total):
+    def step(i, carry):
+        r = start + i
+        shifted = pltpu.roll(rows_ref[r].astype(F32), margin, 1)
+        first = jnp.where(lane < margin, down(shifted), shifted)
+        second = jnp.where(lane < margin, shifted, up(shifted))
+        at = pl.ds(pl.multiple_of(r // 2 * CAP, CAP), CAP)
+        windows[r % 2, at, 0:PW] = first.astype(BF16)
+        windows[r % 2, at, PW:2 * PW] = second.astype(BF16)
+        return carry
+
+    lax.fori_loop(0, count, step, 0, unroll=unroll)
+
+
+def clear_windows(start, count, windows):
+    def step(i, carry):
+        r = start + i
+        at = pl.ds(pl.multiple_of(r // 2 * CAP, CAP), CAP)
+        windows[r % 2, at, :] = jnp.zeros((CAP, 2 * PW), BF16)
+        return carry
+
+    lax.fori_loop(0, count, step, 0)
+
+
+def near_first(i):
+    half = (i + 1) // 2
+    return lax.rem(half * (2 * (i % 2) - 1) + NZ, NZ)
+
+
+def far_first(i):
+    half = (i + 1) // 2
+    return lax.rem(NZ // 2 + half * (1 - 2 * (i % 2)) + NZ, NZ)
+
+
+def banded(windows, bands, per_step, first, last, total):
     half = ROWS // 2 * CAP
-    taps = (extent + 1) // 2
 
     def part(step):
         left = []
@@ -108,23 +131,25 @@
         right = bands[pl.ds(pl.multiple_of(step * depth, depth), depth), :]
         return jnp.dot(jnp.concatenate(left, axis=1), right, preferred_element_type=F32)
 
-    total[...] = part(0)
+    if first == 0:
+        total[...] = part(0)
 
     def step(i, carry):
         total[...] += part(i)
         return carry
 
-    lax.fori_loop(1, taps // per_step, step, 0)
+    lax.fori_loop(max(first, 1), last, step, 0)
 
 
 def kernel(
-    exposure, template, row_shift, column_shift, row_fraction, column_fraction,
-    piece_width, route_tile, route_cell, match_kernel, detection_kernel,
-    difference, significance, noise,
-    ext, hx, tf, tb, rfw, cfw, meta, msg, rcv, agb, acc, outg, grcv,
+    exposure, template, *rest):
+    small, rest = rest[:9], rest[9:]
+    (difference, significance, noise, scale,
+    ext, hx, tf, tb, rfw, cfw, meta, msg, rcv, agb, acc, outg, grcv, held, mfr, mrc,
     base_lo, base_hi, bands, dbands, windows, dwindows, total, matched, diffs, db,
     arsrc, arcv, ar2src, arcv2, local, sends, recvs,
-):
+    row_shift, column_shift, row_fraction, column_fraction,
+    piece_width, route_tile, route_cell, match_kernel, detection_kernel) = rest
     z, x, y = (lax.axis_index(a) for a in CCD)
     c = lax.axis_index("row")
     me = z * NY + y
@@ -153,15 +178,24 @@
     def sent(ref, stage):
         pltpu.make_async_copy(ref, ref, sends.at[stage]).wait()
 
-    for p in range(NP):
-        pltpu.make_async_copy(exposure.at[:, pl.ds(p * PW, PW)], ext.at[pl.ds(0, ROWS), p, :], local.at[0]).start()
-    for q in range(CAP):
-        pltpu.make_async_copy(template.at[:, pl.ds(q * PW, PW)], tf.at[:, q, :], local.at[1]).start()
     barrier = pltpu.get_barrier_semaphore()
     for dz, dy in near:
         pl.semaphore_signal(barrier, inc=1, device_id=zpeer(dz, dy)[2], device_id_type=MESH)
     for dx, dc in across:
         pl.semaphore_signal(barrier, inc=1, device_id=xpeer(dx, dc), device_id_type=MESH)
+    held_small = (
+        row_shift, column_shift, row_fraction, column_fraction,
+        piece_width, route_tile, route_cell, match_kernel, detection_kernel,
+    )
+    loads = [pltpu.make_async_copy(src, dst, local.at[4 + i]) for i, (src, dst) in enumerate(zip(small, held_small))]
+    for load in loads:
+        load.start()
+    for q in range(CAP):
+        pltpu.make_async_copy(template.at[:, pl.ds(q * PW, PW)], tf.at[:, q, :], local.at[1]).start()
+    for p in range(NP):
+        pltpu.make_async_copy(exposure.at[:, pl.ds(p * PW, PW)], ext.at[pl.ds(0, ROWS), p, :], local.at[0]).start()
+    for load in loads:
+        load.wait()
 
     fractions = row_fraction[...].astype(F32)
     for r in range(ROWS):
@@ -174,26 +208,24 @@
     tile16 = column_of(route_tile[...].astype(F32), NP)
     cell16 = column_of(route_cell[...].astype(F32), NP)
     meta[...] = jnp.where(lane16 == 96, tile16, jnp.where(lane16 == 97, cell16, jnp.where(lane16 == 98, width16, 0.0)))
-    build_bands(match_kernel, KS, base_lo, base_hi, bands)
-    margin = KS // 2
+    margin, dmargin = KS // 2, DK // 2
     pltpu.make_async_copy(tf, tf, local.at[1]).wait()
 
     def round_template(r, carry):
         tb[margin + r] = tf[r].astype(BF16)
         return carry
 
-    lax.fori_loop(0, ROWS, round_template, 0)
-
-    def zero_template(r, carry):
-        tb[c * (ROWS + margin) + r] = jnp.zeros((CAP, PW), BF16)
-        return carry
-
-    lax.fori_loop(0, margin, zero_template, 0)
+    lax.fori_loop(0, ROWS, round_template, 0, unroll=4)
+    band_bases(match_kernel, KS, base_lo, base_hi, bands)
+    build_bands(base_lo, base_hi, bands, 0, EARLY)
+    clear_windows(c * (ROWS + margin), margin, windows)
+    clear_windows(c * (ROWS + dmargin), dmargin, dwindows)
     pltpu.make_async_copy(ext.at[pl.ds(0, ROWS)], ext.at[pl.ds(0, ROWS)], local.at[0]).wait()
     pl.semaphore_wait(barrier, len(near) + len(across))
 
     send(ext.at[pl.ds(0, HALO)], hx, 0, partner)
     send(tb.at[pl.ds(margin + (1 - c) * (ROWS - margin), margin)], tb.at[pl.ds(c * (ROWS + margin), margin)], 1, partner)
+    build_windows(tb, margin, ROWS, margin, windows, 4)
     arrived(hx, 0)
     keep = jnp.where(c == 0, 1.0, 0.0)
     for r in range(HALO):
@@ -229,26 +261,44 @@
             out.append(value.astype(BF16))
         return out
 
-    def spread(dz, carry):
-        pz = lax.rem(z + dz, NZ)
-        for py, value in enumerate(fragments(pz)):
-            msg[pz * NY + py] = value
-        for dy in range(NY):
-            _, py, device = zpeer(dz, dy)
-            send(msg.at[pz * NY + py], rcv.at[me], 2, device)
-        return carry
-
-    lax.fori_loop(1, NZ, spread, 0)
+    def spread(slot):
+        def step(i, carry):
+            dz = near_first(i)
+            pz = lax.rem(z + dz, NZ)
+            for py, value in enumerate(fragments(pz)):
+                msg[pz * NY + py] = value
+            for dy in range(NY):
+                _, py, device = zpeer(dz, dy)
+                send(msg.at[pz * NY + py], rcv.at[me], 2, device, slot)
+            return carry
+
+        return step
+
     for py, value in enumerate(fragments(z)):
         msg[z * NY + py] = value
     for dy in range(1, NY):
         _, py, device = zpeer(0, dy)
-        send(msg.at[z * NY + py], rcv.at[me], 2, device)
+        send(msg.at[z * NY + py], rcv.at[me], 2, device, 2)
+    lax.fori_loop(1, 3, spread(2), 0)
+    lax.fori_loop(3, 5, spread(3), 0)
+    lax.fori_loop(5, 8, spread(4), 0)
     rcv[me] = msg[me]
 
-    arrived(hx_template(tb, margin, c), 1)
-    build_windows(tb, ROWS + 2 * margin, margin, windows)
-    banded(windows, bands, KS, 3, total)
+    def forward(slot, distances, count):
+        arrived(rcv.at[pl.ds(0, count)], slot)
+        for dz in distances:
+            at = pl.ds(lax.rem(z + dz, NZ) * NY, NY)
+            for dx in (2, 1, 3):
+                send(rcv.at[at], agb.at[dx - 1, at], 3, xpeer(dx), slot=9 + dx)
+
+    arrived(other_rows(tb, margin, c), 1)
+    build_windows(tb, (1 - c) * (ROWS + margin), margin, margin, windows, 4)
+    build_bands(base_lo, base_hi, bands, EARLY, KS)
+    forward(2, (0, 1, 7), 11)
+    banded(windows, bands, 3, 0, 3, total)
+    forward(3, (2, 6), 8)
+    banded(windows, bands, 3, 3, 7, total)
+    forward(4, (3, 5, 4), 12)
 
     def unpair(q, carry):
         at = pl.ds(pl.multiple_of(q * CAP, CAP), CAP)
@@ -256,12 +306,37 @@
         matched[2 * q + 1] = total[at, PW:2 * PW]
         return carry
 
-    lax.fori_loop(0, ROWS // 2, unpair, 0)
-    build_bands(detection_kernel, DK, base_lo, base_hi, dbands)
-    arrived(rcv.at[pl.ds(0, GROUP - 1)], 2)
-
-    for dx in (1, 3, 2):
-        send(rcv, agb.at[dx - 1], 3, xpeer(dx), slot=8 + dx)
+    lax.fori_loop(0, ROWS // 2, unpair, 0, unroll=2)
+    lane24 = lanes_of((ROWS, PW))
+
+    def split(pz):
+        for py in range(NY):
+            value, last = None, []
+            for j in range(FR):
+                turn = (FL * (j - py)) % PW
+                row = matched[pz * FR + j]
+                moved = pltpu.roll(row[:ROWS], turn, 1) if turn else row[:ROWS]
+                value = moved if value is None else jnp.where(lane24 >= FL * j, moved, value)
+                turn = (FL * (FR - py)) % PW
+                last.append(pltpu.roll(row[ROWS:], turn, 1) if turn else row[ROWS:])
+            value = jnp.where(lane24 >= FR * FL, jnp.concatenate(last, axis=0), value)
+            mfr[pz * NY + py] = value.astype(BF16)
+
+    def follow(i, carry):
+        dz = far_first(i)
+        pz = lax.rem(z + dz, NZ)
+        split(pz)
+        for dy in range(NY):
+            _, py, device = zpeer(dz, dy)
+            send(mfr.at[pz * NY + py], mrc.at[me], 4, device, 5)
+        return carry
+
+    lax.fori_loop(0, NZ - 1, follow, 0)
+    split(z)
+    for dy in range(1, NY):
+        _, py, device = zpeer(0, dy)
+        send(mfr.at[z * NY + py], mrc.at[me], 4, device, 5)
+    mrc[me] = mfr[me]
 
     def codes(block):
         picks = (lanes_of((8, PW)) == lax.broadcasted_iota(I32, (8, PW), 0) + 96).astype(F32).astype(BF16)
@@ -290,120 +365,166 @@
             acc[at, :] = value if first else acc[at, :] + value
             return carry
 
-        lax.fori_loop(0, NZ, step, 0)
+        lax.fori_loop(0, NZ, step, 0, unroll=8)
 
     add_block(flat(rcv), True)
-    arrived(agb.at[0], 9)
+    arrived(agb.at[2], 12)
+    add_block(flat(agb.at[2]), False)
+    arrived(agb.at[0], 10)
     add_block(flat(agb.at[0]), False)
-    arrived(agb.at[2], 11)
-    add_block(flat(agb.at[2]), False)
-    arrived(agb.at[1], 10)
+    arrived(agb.at[1], 11)
     block = flat(agb.at[1])
     code = codes(block)
 
+    lane8 = lanes_of((8, PW))
+
     def finish(pz):
         at = pl.ds(pl.multiple_of(pz * chunk, chunk), chunk)
-        value = (acc[at, :] + chosen(code, block, pz)).astype(BF16)
+        value = acc[at, :] + chosen(code, block, pz)
+        acc[at, :] = value
         for py in range(NY):
-            outg[pz * NY + py] = value[py * CAP:(py + 1) * CAP]
-
-    def deliver(dz, carry):
+            tile = value[py * CAP:(py + 1) * CAP]
+            rows = []
+            for j in range(FR):
+                turn = (FL * (FR - j)) % PW
+                rows.append(jnp.where(lane8 >= FR * FL, pltpu.roll(tile[ROWS:], turn, 1), tile[8 * j:8 * j + 8]))
+            outg[pz * NY + py] = jnp.concatenate(rows, axis=0).astype(BF16)
+        return value
+
+    def deliver(i, carry):
+        dz = far_first(i)
         pz = lax.rem(z + dz, NZ)
         finish(pz)
         for dy in range(NY):
             _, py, device = zpeer(dz, dy)
-            send(outg.at[pz * NY + py], grcv.at[me], 4, device)
-        return carry
-
-    lax.fori_loop(1, NZ, deliver, 0)
-    finish(z)
+            send(outg.at[pz * NY + py], grcv.at[me], 5, device, 6)
+        return carry
+
+    lax.fori_loop(0, NZ - 1, deliver, 0, unroll=7)
+    held[...] = finish(z)
     for dy in range(1, NY):
         _, py, device = zpeer(0, dy)
-        send(outg.at[z * NY + py], grcv.at[me], 4, device)
+        send(outg.at[z * NY + py], grcv.at[me], 5, device, 6)
     grcv[me] = outg[me]
+
+    lane32 = lanes_of((CAP, PW))
+    own = held[pl.ds(pl.multiple_of(y * CAP, CAP), CAP), :]
+    width32 = jnp.sum(jnp.where(lane32 == 98, own, 0.0), axis=1, keepdims=True)
+    live = lane32.astype(F32) < width32
+    live_count = ROWS * jnp.sum(width32, axis=0, keepdims=True)
+    place = (lax.rem(lane24, FL) + FL * y).astype(F32)
+    arrived(mrc.at[pl.ds(0, GROUP - 1)], 5)
+
+    def square(k, squares):
+        value = acc[pl.ds(pl.multiple_of(k * CAP, CAP), CAP), :]
+        width = jnp.sum(jnp.where(lane32 == 98, value, 0.0), axis=1, keepdims=True)
+        last = jnp.concatenate([width[ROWS:]] * FR, axis=0)
+        width = jnp.where(lane24 < FR * FL, width[:ROWS], last)
+        value = jnp.where(place < width, outg[k].astype(F32) - mrc[k].astype(F32), 0.0)
+        return squares + value * value
+
+    squares = lax.fori_loop(0, GROUP, square, jnp.zeros((ROWS, PW), F32), unroll=4)
+    square_sum = jnp.sum(jnp.sum(squares, axis=1, keepdims=True), axis=0, keepdims=True)
+    lane1 = lanes_of((1, PW))
+    arsrc[...] = jnp.where(lane1 == 0, square_sum, jnp.where(lane1 == 1, live_count, 0.0))
+    for dz, dy in near:
+        send(arsrc, arcv.at[me], 6, zpeer(dz, dy)[2], 7)
+    arcv[me] = arsrc[...]
+    band_bases(detection_kernel, DK, base_lo, base_hi, dbands)
+    build_bands(base_lo, base_hi, dbands, 0, DK)
     sent(rcv.at[pl.ds(0, GROUP - 1)], 2)
     sent(agb, 3)
     sent(hx, 0)
     sent(tb.at[pl.ds(0, margin)], 1)
-
-    dmargin = DK // 2
-
-    def zero_difference(r, carry):
-        db[c * (ROWS + dmargin) + r] = jnp.zeros((CAP, PW), BF16)
-        return carry
-
-    lax.fori_loop(0, dmargin, zero_difference, 0)
-    arrived(grcv.at[pl.ds(0, GROUP - 1)], 4)
-
-    lane32 = lanes_of((CAP, PW))
-    own = grcv[me].astype(F32)
-    width32 = jnp.sum(jnp.where(lane32 == 98, own, 0.0), axis=1, keepdims=True)
-    live = lane32.astype(F32) < width32
-
-    def subtract(pz, squares):
+    sent(mrc.at[pl.ds(0, GROUP - 1)], 4)
+    arrived(grcv.at[pl.ds(0, GROUP - 1)], 6)
+
+    def subtract(pz, carry):
         parts = [grcv[pz * NY + py].astype(F32) for py in range(NY)]
         for j in range(FR):
             science = None
             for py in range(NY):
                 turn = (FL * (py - j)) % PW
                 moved = pltpu.roll(parts[py], turn, 1) if turn else parts[py]
+                turn = (FL * (py - FR)) % PW
+                rest = parts[py][8 * j:8 * j + 8]
+                rest = pltpu.roll(rest, turn, 1) if turn else rest
+                moved = jnp.concatenate([moved, rest], axis=0)
                 science = moved if science is None else jnp.where(lane32 >= FL * py, moved, science)
             r = pz * FR + j
             value = jnp.where(live, science - matched[r], 0.0)
             diffs[r] = value
             db[dmargin + r] = value.astype(BF16)
-            squares = squares + value * value
-        return squares
-
-    squares = lax.fori_loop(0, NZ, subtract, jnp.zeros((CAP, PW), F32))
-    square_sum = jnp.sum(jnp.sum(squares, axis=1, keepdims=True), axis=0, keepdims=True)
-    live_count = ROWS * jnp.sum(width32, axis=0, keepdims=True)
-    lane1 = lanes_of((1, PW))
-    arsrc[...] = jnp.where(lane1 == 0, square_sum, jnp.where(lane1 == 1, live_count, 0.0))
-    for dz, dy in near:
-        send(arsrc, arcv.at[me], 5, zpeer(dz, dy)[2])
-    arcv[me] = arsrc[...]
-    send(db.at[pl.ds(dmargin + (1 - c) * (ROWS - dmargin), dmargin)], db.at[pl.ds(c * (ROWS + dmargin), dmargin)], 6, partner)
+        return carry
+
+    lax.fori_loop(0, NZ, subtract, 0)
+    send(db.at[pl.ds(dmargin + (1 - c) * (ROWS - dmargin), dmargin)], db.at[pl.ds(c * (ROWS + dmargin), dmargin)], 8, partner, 9)
     for q in range(CAP):
         pltpu.make_async_copy(diffs.at[:, q, :], difference.at[:, pl.ds(q * PW, PW)], local.at[2]).start()
-    arrived(hx_template(db, dmargin, c), 6)
-
-    build_windows(db, ROWS + 2 * dmargin, dmargin, dwindows)
-    banded(dwindows, dbands, DK, 2, total)
-    arrived(arcv.at[pl.ds(0, GROUP - 1)], 5)
+    build_windows(db, dmargin, ROWS, dmargin, dwindows, 4)
+    arrived(arcv.at[pl.ds(0, GROUP - 1)], 7)
     ar2src[...] = jnp.sum(arcv[...], axis=0)
     for dx, dc in across:
-        send(ar2src, arcv2.at[x * 2 + c], 7, xpeer(dx, dc))
+        send(ar2src, arcv2.at[x * 2 + c], 7, xpeer(dx, dc), 8)
     arcv2[x * 2 + c] = ar2src[...]
-    arrived(arcv2.at[pl.ds(0, 7)], 7)
+
+    arrived(other_rows(db, dmargin, c), 9)
+    build_windows(db, (1 - c) * (ROWS + dmargin), dmargin, dmargin, dwindows, 7)
+    banded(dwindows, dbands, 2, 0, (DK + 1) // 4, total)
+
+    def unpair_filtered(q, carry):
+        at = pl.ds(pl.multiple_of(q * CAP, CAP), CAP)
+        tf[2 * q] = total[at, 0:PW]
+        tf[2 * q + 1] = total[at, PW:2 * PW]
+        return carry
+
+    lax.fori_loop(0, ROWS // 2, unpair_filtered, 0, unroll=2)
+    for q in range(CAP):
+        pltpu.make_async_copy(tf.at[:, q, :], significance.at[:, pl.ds(q * PW, PW)], local.at[3]).start()
+    arrived(arcv2.at[pl.ds(0, 7)], 8)
     sums = jnp.sum(arcv2[...], axis=0)
     whole_square = jnp.sum(jnp.where(lane1 == 0, sums, 0.0), axis=1, keepdims=True)
     whole_count = jnp.sum(jnp.where(lane1 == 1, sums, 0.0), axis=1, keepdims=True)
     level = whole_square / whole_count
     taps = detection_kernel[...].astype(F32)
     norm = jnp.sum(jnp.sum(taps * taps, axis=1, keepdims=True), axis=0, keepdims=True)
-    scale = jnp.broadcast_to(1.0 / jnp.sqrt(1.0 + level * norm), (CAP, PW))
     noise[...] = jnp.broadcast_to(level, (1, PW))
-
-    def rescale(q, carry):
-        at = pl.ds(pl.multiple_of(q * CAP, CAP), CAP)
-        tf[2 * q] = total[at, 0:PW] * scale
-        tf[2 * q + 1] = total[at, PW:2 * PW] * scale
-        return carry
-
-    lax.fori_loop(0, ROWS // 2, rescale, 0)
-    for q in range(CAP):
-        pltpu.make_async_copy(tf.at[:, q, :], significance.at[:, pl.ds(q * PW, PW)], local.at[3]).start()
-    sent(grcv.at[pl.ds(0, GROUP - 1)], 4)
-    sent(arcv.at[pl.ds(0, GROUP - 1)], 5)
-    sent(db.at[pl.ds(0, dmargin)], 6)
+    scale[...] = jnp.broadcast_to(1.0 / jnp.sqrt(1.0 + level * norm), (1, PW))
+    sent(grcv.at[pl.ds(0, GROUP - 1)], 5)
+    sent(arcv.at[pl.ds(0, GROUP - 1)], 6)
     sent(arcv2.at[pl.ds(0, 7)], 7)
+    sent(db.at[pl.ds(0, dmargin)], 8)
     pltpu.make_async_copy(diffs, diffs, local.at[2]).wait()
     pltpu.make_async_copy(tf, tf, local.at[3]).wait()
 
 
-def hx_template(ref, margin, c):
+def other_rows(ref, margin, c):
     return ref.at[pl.ds((1 - c) * (ROWS + margin), margin)]
+
+
+def finish_kernel(difference, filtered, level, scale, out_difference, out_significance, noise, held, sums, factor, total, ins, outs):
+    parts = [slice(r, r + 8) for r in range(0, ROWS, 8)]
+    loads = [pltpu.make_async_copy(scale, factor, ins.at[0])]
+    loads += [pltpu.make_async_copy(filtered.at[at], sums.at[at], ins.at[1 + i]) for i, at in enumerate(parts)]
+    loads += [pltpu.make_async_copy(difference.at[at], held.at[at], ins.at[4 + i]) for i, at in enumerate(parts)]
+    loads += [pltpu.make_async_copy(level, total, ins.at[7])]
+    for load in loads:
+        load.start()
+    loads[0].wait()
+    stores = []
+    for i, at in enumerate(parts):
+        loads[1 + i].wait()
+        sums[at] = sums[at] * factor[0:1, 0:1]
+        stores.append(pltpu.make_async_copy(sums.at[at], out_significance.at[at], outs.at[i]))
+        stores[-1].start()
+    for i, at in enumerate(parts):
+        loads[4 + i].wait()
+        stores.append(pltpu.make_async_copy(held.at[at], out_difference.at[at], outs.at[3 + i]))
+        stores[-1].start()
+    loads[7].wait()
+    noise[...] = total[...]
+    for store in stores:
+        store.wait()
 
 
 def on_device(
@@ -411,19 +532,19 @@
     route_tile, route_cell, template, match_kernel, detection_kernel,
 ):
     vmem = pl.BlockSpec(memory_space=pltpu.VMEM)
-    smem = pl.BlockSpec(memory_space=pltpu.SMEM)
     far = pl.BlockSpec(memory_space=pl.ANY)
     wide = template.shape[2]
     margin, dmargin = KS // 2, DK // 2
-    difference, significance, noise = pl.pallas_call(
+    difference, filtered, noise, scale = pl.pallas_call(
         kernel,
         out_shape=(
             jax.ShapeDtypeStruct((ROWS, wide), F32),
             jax.ShapeDtypeStruct((ROWS, wide), F32),
             jax.ShapeDtypeStruct((1, PW), F32),
+            jax.ShapeDtypeStruct((1, PW), F32),
         ),
-        in_specs=[far, far, smem, smem] + [vmem] * 7,
-        out_specs=(far, far, vmem),
+        in_specs=[far] * 11,
+        out_specs=(far, far, vmem, vmem),
         scratch_shapes=[
             pltpu.VMEM((ROWS + HALO, NP, PW), F32),
             pltpu.VMEM((HALO, NP, PW), F32),
@@ -436,8 +557,11 @@
             pltpu.VMEM((GROUP, NP, PW), BF16),
             pltpu.VMEM((NX - 1, GROUP, NP, PW), BF16),
             pltpu.VMEM((GROUP * CAP, PW), F32),
-            pltpu.VMEM((GROUP, CAP, PW), BF16),
-            pltpu.VMEM((GROUP, CAP, PW), BF16),
+            pltpu.VMEM((GROUP, ROWS, PW), BF16),
+            pltpu.VMEM((GROUP, ROWS, PW), BF16),
+            pltpu.VMEM((NY * CAP, PW), F32),
+            pltpu.VMEM((GROUP, ROWS, PW), BF16),
+            pltpu.VMEM((GROUP, ROWS, PW), BF16),
             pltpu.VMEM((48 * 8, PW), F32),
             pltpu.VMEM((48 * 8, PW), F32),
             pltpu.VMEM(((KS + 1) * 2 * PW, 2 * PW), BF16),
@@ -452,9 +576,18 @@
             pltpu.VMEM((GROUP, 1, PW), F32),
             pltpu.VMEM((1, PW), F32),
             pltpu.VMEM((8, 1, PW), F32),
-            pltpu.SemaphoreType.DMA((4,)),
-            pltpu.SemaphoreType.DMA((8,)),
-            pltpu.SemaphoreType.DMA((12,)),
+            pltpu.SemaphoreType.DMA((13,)),
+            pltpu.SemaphoreType.DMA((9,)),
+            pltpu.SemaphoreType.DMA((13,)),
+            pltpu.SMEM((1,), I32),
+            pltpu.SMEM((1,), I32),
+            pltpu.VMEM((1, ROWS), BF16),
+            pltpu.VMEM((1, NP * PW), BF16),
+            pltpu.VMEM((1, NP), I32),
+            pltpu.VMEM((1, NP), I32),
+            pltpu.VMEM((1, NP), I32),
+            pltpu.VMEM((KS, KS), BF16),
+            pltpu.VMEM((DK, DK), BF16),
         ],
         compiler_params=pltpu.CompilerParams(collective_id=0, has_side_effects=True, vmem_limit_bytes=60 * 1024 * 1024),
         name="warp_match_detect",
@@ -462,6 +595,26 @@
         exposure[0], template[0], row_shift, column_shift, row_fraction, column_fraction,
         piece_width, route_tile, route_cell, match_kernel[0], detection_kernel[0],
     )
+    difference, significance, noise = pl.pallas_call(
+        finish_kernel,
+        out_shape=(
+            jax.ShapeDtypeStruct((ROWS, wide), F32),
+            jax.ShapeDtypeStruct((ROWS, wide), F32),
+            jax.ShapeDtypeStruct((1, PW), F32),
+        ),
+        in_specs=[far] * 4,
+        out_specs=(far, far, vmem),
+        scratch_shapes=[
+            pltpu.VMEM((ROWS, wide), F32),
+            pltpu.VMEM((ROWS, wide), F32),
+            pltpu.VMEM((1, PW), F32),
+            pltpu.VMEM((1, PW), F32),
+            pltpu.SemaphoreType.DMA((8,)),
+            pltpu.SemaphoreType.DMA((6,)),
+        ],
+        compiler_params=pltpu.CompilerParams(vmem_limit_bytes=60 * 1024 * 1024),
+        name="finish",
+    )(difference, filtered, noise, scale)
     return difference[None], significance[None], noise[0, 0]
 
 

time: 58.8 us -> 45.6 us (0.78)
  Pallas kernels: 52.9 us -> 43.5 us
  local copies, waits for them, and re-layouts: 2.57 us -> 0 us
  between operations: 3.11 us -> 1.93 us
    pallas_call x1, Pallas kernels: 52.9 us -> 40.9 us  [on_device(): pl.pallas_call(kernel, out_shape=(jax.ShapeDtypeStruct((ROWS, wide), F32)...]
    unnamed x6 -> x0, local copies, waits for them, and re-layouts: 2.57 us -> none
    pallas_call x0 -> x1, Pallas kernels: none -> 2.56 us  [on_device(): pl.pallas_call(finish_kernel, out_shape=(jax.ShapeDtypeStruct((ROWS, wide...]
where the time goes in v2:
time: 45.6 us; the launch traced here: 45.4 us
  Pallas kernels  43.5 us (95%)
  between operations  1.93 us (4%)
    pallas_call x1, Pallas kernels, on_device(): pl.pallas_call(kernel, out_shape=(jax.ShapeDtypeStruct((ROWS, wide), F32)...  40.9 us
    pallas_call x1, Pallas kernels, on_device(): pl.pallas_call(finish_kernel, out_shape=(jax.ShapeDtypeStruct((ROWS, wide...  2.56 us

profile of v2, /device:TPU:1, one launch (start us, length us, event | category | flops | bytes accessed | tf_op | source)
XLA Modules:
  0.0 45.4 jit_solution(10619232868609477232)
XLA Ops:
  1.9 40.9 %warp_match_detect.1 = (f32[24,4096]{1,0:T(8,128)}, f32[24,4096]{1,0:T(8,128)}, f32[1,128]{1,0:T(1,128)}, f32[1,128]{1,0:T(1,128)}) custom-call(f32[24,2048]{1,0:T(8,128)} %bitcast.9, f32[24,4096]{1,0:T(8,128)} %bitcast.8, s32[1]{0:T(128)S(6)} %copy.14.rest_0_, s32[1]{0:T(128)S(6)} %copy.15.rest_1_, bf16[1,24]{1,0:T(2,128)(2,1)} %rest_2_.1, ...), custom_call_target="tpu_custom_call" | custom-call | tf_op jit(solution)/shard_map/warp_match_detect/pallas_call | solution.py:538
  42.8 2.6 %finish.1 = (f32[24,4096]{1,0:T(8,128)}, f32[24,4096]{1,0:T(8,128)}, f32[1,128]{1,0:T(1,128)}) custom-call(f32[24,4096]{1,0:T(8,128)} %get-tuple-element.10.difference, f32[24,4096]{1,0:T(8,128)} %get-tuple-element.11.filtered, f32[1,128]{1,0:T(1,128)} %get-tuple-element.12.level, f32[1,128]{1,0:T(1,128)} %get-tuple-element.13.scale), custom_call_target="tpu_custom_call" | custom-call | tf_op jit(solution)/shard_map/finish/pallas_call | solution.py:598

commit v3 on v2

--- a/solution.py
+++ b/solution.py
@@ -19,7 +19,7 @@
 ROWS = 24
 FR = ROWS // NZ
 FL = PW // NY
-EARLY = 18
+EARLY = 5
 MESH = pl.DeviceIdType.MESH
 CCD = ("ccd_0", "ccd_1", "ccd_2")
 F32, BF16, I32 = jnp.float32, jnp.bfloat16, jnp.int32
@@ -54,11 +54,11 @@
         rolled = pltpu.roll(turned, s, 1) if s else turned
         base_lo[pl.ds(s, extent, stride=8), :] = rolled[:, :PW]
         base_hi[pl.ds(s, extent, stride=8), :] = rolled[:, PW:]
-    bands[0:2 * PW, PW:] = jnp.zeros((2 * PW, PW), BF16)
-    bands[extent * 2 * PW:(extent + 1) * 2 * PW, :PW] = jnp.zeros((2 * PW, PW), BF16)
-
-
-def build_bands(base_lo, base_hi, bands, first, last):
+    bands[0:2 * PW, :] = jnp.zeros((2 * PW, PW), BF16)
+    bands[(extent + 1) * 2 * PW:(extent + 2) * 2 * PW, :] = jnp.zeros((2 * PW, PW), BF16)
+
+
+def build_bands(base_lo, base_hi, bands, extent, unroll):
     lane = lanes_of((8, PW))
 
     def step(a, carry):
@@ -73,14 +73,11 @@
                 near.append(jnp.where(lane >= shift, rlo, rhi))
                 far.append(jnp.where(lane >= shift, rhi, rlo))
             for value, start in ((near, 16 * pair), (far, PW + 16 * pair)):
-                block = jnp.concatenate(value, axis=0).astype(BF16)
-                at = pl.multiple_of(a * 2 * PW + start, 16)
-                bands[pl.ds(at, 16), 0:PW] = block
-                after = pl.multiple_of((a + 1) * 2 * PW + start, 16)
-                bands[pl.ds(after, 16), PW:2 * PW] = block
-        return carry
-
-    lax.fori_loop(first, last, step, 0)
+                at = pl.multiple_of((a + 1) * 2 * PW + start, 16)
+                bands[pl.ds(at, 16), :] = jnp.concatenate(value, axis=0).astype(BF16)
+        return carry
+
+    lax.fori_loop(0, extent, step, 0, unroll=unroll)
 
 
 def build_windows(rows_ref, start, count, margin, windows, unroll):
@@ -128,7 +125,8 @@
             at = pl.ds(pl.multiple_of((step * per_step + i) * CAP, CAP), half)
             left += [windows[0, at, :], windows[1, at, :]]
         depth = per_step * 4 * PW
-        right = bands[pl.ds(pl.multiple_of(step * depth, depth), depth), :]
+        at = pl.multiple_of(step * depth, depth)
+        right = jnp.concatenate([bands[pl.ds(at + 2 * PW, depth), :], bands[pl.ds(at, depth), :]], axis=1)
         return jnp.dot(jnp.concatenate(left, axis=1), right, preferred_element_type=F32)
 
     if first == 0:
@@ -143,13 +141,12 @@
 
 def kernel(
     exposure, template, *rest):
-    small, rest = rest[:9], rest[9:]
-    (difference, significance, noise, scale,
-    ext, hx, tf, tb, rfw, cfw, meta, msg, rcv, agb, acc, outg, grcv, held, mfr, mrc,
+    row_shift, column_shift, small, rest = *rest[:2], rest[2:9], rest[9:]
+    (difference, significance, stats,
+    ext, hx, tf, tb, rfw, cfw, meta, msg, rcv, agb, acc, outg, grcv, held, mfr, mrc, alive,
     base_lo, base_hi, bands, dbands, windows, dwindows, total, matched, diffs, db,
-    arsrc, arcv, ar2src, arcv2, local, sends, recvs,
-    row_shift, column_shift, row_fraction, column_fraction,
-    piece_width, route_tile, route_cell, match_kernel, detection_kernel) = rest
+    arsrc, arcv, ar2src, arcv2, numbers, local, sends, recvs,
+    row_fraction, column_fraction, piece_width, route_tile, route_cell, match_kernel, detection_kernel) = rest
     z, x, y = (lax.axis_index(a) for a in CCD)
     c = lax.axis_index("row")
     me = z * NY + y
@@ -184,8 +181,7 @@
     for dx, dc in across:
         pl.semaphore_signal(barrier, inc=1, device_id=xpeer(dx, dc), device_id_type=MESH)
     held_small = (
-        row_shift, column_shift, row_fraction, column_fraction,
-        piece_width, route_tile, route_cell, match_kernel, detection_kernel,
+        row_fraction, column_fraction, piece_width, route_tile, route_cell, match_kernel, detection_kernel,
     )
     loads = [pltpu.make_async_copy(src, dst, local.at[4 + i]) for i, (src, dst) in enumerate(zip(small, held_small))]
     for load in loads:
@@ -217,22 +213,12 @@
 
     lax.fori_loop(0, ROWS, round_template, 0, unroll=4)
     band_bases(match_kernel, KS, base_lo, base_hi, bands)
-    build_bands(base_lo, base_hi, bands, 0, EARLY)
+    build_bands(base_lo, base_hi, bands, KS, 4)
     clear_windows(c * (ROWS + margin), margin, windows)
     clear_windows(c * (ROWS + dmargin), dmargin, dwindows)
     pltpu.make_async_copy(ext.at[pl.ds(0, ROWS)], ext.at[pl.ds(0, ROWS)], local.at[0]).wait()
-    pl.semaphore_wait(barrier, len(near) + len(across))
-
-    send(ext.at[pl.ds(0, HALO)], hx, 0, partner)
-    send(tb.at[pl.ds(margin + (1 - c) * (ROWS - margin), margin)], tb.at[pl.ds(c * (ROWS + margin), margin)], 1, partner)
-    build_windows(tb, margin, ROWS, margin, windows, 4)
-    arrived(hx, 0)
-    keep = jnp.where(c == 0, 1.0, 0.0)
-    for r in range(HALO):
-        ext[ROWS + r] = hx[r] * keep
-
-    t = row_shift[0]
-    s = column_shift[0]
+    t = jnp.max(row_shift[...].reshape(1, 1))
+    s = jnp.max(column_shift[...].reshape(1, 1))
     left_turn = lax.rem(PW - s, PW)
     right_turn = PW - 1 - s
     weight = cfw[...]
@@ -261,43 +247,71 @@
             out.append(value.astype(BF16))
         return out
 
-    def spread(slot):
-        def step(i, carry):
-            dz = near_first(i)
-            pz = lax.rem(z + dz, NZ)
-            for py, value in enumerate(fragments(pz)):
-                msg[pz * NY + py] = value
-            for dy in range(NY):
-                _, py, device = zpeer(dz, dy)
-                send(msg.at[pz * NY + py], rcv.at[me], 2, device, slot)
-            return carry
-
-        return step
-
-    for py, value in enumerate(fragments(z)):
-        msg[z * NY + py] = value
-    for dy in range(1, NY):
-        _, py, device = zpeer(0, dy)
-        send(msg.at[z * NY + py], rcv.at[me], 2, device, 2)
-    lax.fori_loop(1, 3, spread(2), 0)
-    lax.fori_loop(3, 5, spread(3), 0)
-    lax.fori_loop(5, 8, spread(4), 0)
+    def place_fragments(pz):
+        for py, value in enumerate(fragments(pz)):
+            msg[pz * NY + py] = value
+
+    def spread(pz):
+        d = lax.rem(pz - z + NZ, NZ)
+        dist = d + (NZ - 2 * d) * (d // 5)
+        slot = 2 + (dist + 6) // 8 + (dist + 5) // 8
+        for dy in range(NY):
+            py = lax.rem(y + dy, NY)
+
+            def go():
+                send(msg.at[pz * NY + py], rcv.at[me], 2, {"ccd_0": pz, "ccd_2": py}, slot)
+
+            if dy:
+                go()
+            else:
+                pl.when(z != pz)(go)
+
+    for pz in range(EARLY):
+        place_fragments(pz)
+    pl.semaphore_wait(barrier, len(near) + len(across))
+
+    send(ext.at[pl.ds(0, HALO)], hx, 0, partner)
+    send(tb.at[pl.ds(margin + (1 - c) * (ROWS - margin), margin)], tb.at[pl.ds(c * (ROWS + margin), margin)], 1, partner)
+    for pz in range(EARLY):
+        spread(pz)
+    build_windows(tb, margin, ROWS, margin, windows, 4)
+    arrived(hx, 0)
+    keep = jnp.where(c == 0, 1.0, 0.0)
+    for r in range(HALO):
+        ext[ROWS + r] = hx[r] * keep
+
+    for pz in range(EARLY, NZ):
+        place_fragments(pz)
+        spread(pz)
     rcv[me] = msg[me]
 
     def forward(slot, distances, count):
         arrived(rcv.at[pl.ds(0, count)], slot)
         for dz in distances:
             at = pl.ds(lax.rem(z + dz, NZ) * NY, NY)
-            for dx in (2, 1, 3):
-                send(rcv.at[at], agb.at[dx - 1, at], 3, xpeer(dx), slot=9 + dx)
+            send(rcv.at[at], agb.at[0, at], 3, xpeer(1), slot=slot + 8)
+            send(rcv.at[at], agb.at[2, at], 3, xpeer(3), slot=slot + 11)
+            if slot > 2:
+                send(rcv.at[at], agb.at[1, at], 3, xpeer(2), slot=16)
+
+    def beside(group, count):
+        taken = pl.ds(0, count * NY)
+        arrived(agb.at[0, taken], 10 + group)
+        arrived(agb.at[2, taken], 13 + group)
+
+    def relay(distances):
+        for dz in distances:
+            start = lax.rem(z + dz, NZ) * NY
+            low, high = pl.ds(start, NY // 2), pl.ds(start + NY // 2, NY // 2)
+            send(agb.at[0, low], agb.at[1, low], 3, xpeer(1), slot=16)
+            send(agb.at[2, high], agb.at[1, high], 3, xpeer(3), slot=16)
 
     arrived(other_rows(tb, margin, c), 1)
     build_windows(tb, (1 - c) * (ROWS + margin), margin, margin, windows, 4)
-    build_bands(base_lo, base_hi, bands, EARLY, KS)
+    banded(windows, bands, 3, 0, 4, total)
     forward(2, (0, 1, 7), 11)
-    banded(windows, bands, 3, 0, 3, total)
+    banded(windows, bands, 3, 4, 7, total)
     forward(3, (2, 6), 8)
-    banded(windows, bands, 3, 3, 7, total)
     forward(4, (3, 5, 4), 12)
 
     def unpair(q, carry):
@@ -331,7 +345,7 @@
             send(mfr.at[pz * NY + py], mrc.at[me], 4, device, 5)
         return carry
 
-    lax.fori_loop(0, NZ - 1, follow, 0)
+    lax.fori_loop(0, NZ - 1, follow, 0, unroll=7)
     split(z)
     for dy in range(1, NY):
         _, py, device = zpeer(0, dy)
@@ -368,14 +382,15 @@
         lax.fori_loop(0, NZ, step, 0, unroll=8)
 
     add_block(flat(rcv), True)
-    arrived(agb.at[2], 12)
+    beside(0, 3)
+    relay((0, 1, 7))
+    beside(1, 2)
+    beside(2, 3)
     add_block(flat(agb.at[2]), False)
-    arrived(agb.at[0], 10)
     add_block(flat(agb.at[0]), False)
-    arrived(agb.at[1], 11)
+    arrived(agb.at[1], 16)
     block = flat(agb.at[1])
     code = codes(block)
-
     lane8 = lanes_of((8, PW))
 
     def finish(pz):
@@ -413,30 +428,41 @@
     live = lane32.astype(F32) < width32
     live_count = ROWS * jnp.sum(width32, axis=0, keepdims=True)
     place = (lax.rem(lane24, FL) + FL * y).astype(F32)
-    arrived(mrc.at[pl.ds(0, GROUP - 1)], 5)
-
-    def square(k, squares):
+
+    def mark_live(k, carry):
         value = acc[pl.ds(pl.multiple_of(k * CAP, CAP), CAP), :]
         width = jnp.sum(jnp.where(lane32 == 98, value, 0.0), axis=1, keepdims=True)
         last = jnp.concatenate([width[ROWS:]] * FR, axis=0)
         width = jnp.where(lane24 < FR * FL, width[:ROWS], last)
-        value = jnp.where(place < width, outg[k].astype(F32) - mrc[k].astype(F32), 0.0)
+        alive[k] = jnp.where(place < width, 1.0, 0.0)
+        return carry
+
+    lax.fori_loop(0, GROUP, mark_live, 0, unroll=8)
+    arrived(mrc.at[pl.ds(0, GROUP - 1)], 5)
+
+    def square(k, squares):
+        value = (outg[k].astype(F32) - mrc[k].astype(F32)) * alive[k]
         return squares + value * value
 
-    squares = lax.fori_loop(0, GROUP, square, jnp.zeros((ROWS, PW), F32), unroll=4)
+    squares = lax.fori_loop(0, GROUP, square, jnp.zeros((ROWS, PW), F32), unroll=8)
     square_sum = jnp.sum(jnp.sum(squares, axis=1, keepdims=True), axis=0, keepdims=True)
     lane1 = lanes_of((1, PW))
     arsrc[...] = jnp.where(lane1 == 0, square_sum, jnp.where(lane1 == 1, live_count, 0.0))
-    for dz, dy in near:
-        send(arsrc, arcv.at[me], 6, zpeer(dz, dy)[2], 7)
-    arcv[me] = arsrc[...]
+    for dx, dc in across:
+        send(arsrc, arcv2.at[x * 2 + c], 6, xpeer(dx, dc), 7)
+    arcv2[x * 2 + c] = arsrc[...]
     band_bases(detection_kernel, DK, base_lo, base_hi, dbands)
-    build_bands(base_lo, base_hi, dbands, 0, DK)
+    build_bands(base_lo, base_hi, dbands, DK, 5)
     sent(rcv.at[pl.ds(0, GROUP - 1)], 2)
     sent(agb, 3)
     sent(hx, 0)
     sent(tb.at[pl.ds(0, margin)], 1)
     sent(mrc.at[pl.ds(0, GROUP - 1)], 4)
+    arrived(arcv2.at[pl.ds(0, 7)], 7)
+    ar2src[...] = jnp.sum(arcv2[...], axis=0)
+    for dz, dy in near:
+        send(ar2src, arcv.at[me], 7, zpeer(dz, dy)[2], 8)
+    arcv[me] = ar2src[...]
     arrived(grcv.at[pl.ds(0, GROUP - 1)], 6)
 
     def subtract(pz, carry):
@@ -457,20 +483,15 @@
             db[dmargin + r] = value.astype(BF16)
         return carry
 
-    lax.fori_loop(0, NZ, subtract, 0)
+    lax.fori_loop(0, NZ, subtract, 0, unroll=4)
     send(db.at[pl.ds(dmargin + (1 - c) * (ROWS - dmargin), dmargin)], db.at[pl.ds(c * (ROWS + dmargin), dmargin)], 8, partner, 9)
     for q in range(CAP):
         pltpu.make_async_copy(diffs.at[:, q, :], difference.at[:, pl.ds(q * PW, PW)], local.at[2]).start()
     build_windows(db, dmargin, ROWS, dmargin, dwindows, 4)
-    arrived(arcv.at[pl.ds(0, GROUP - 1)], 7)
-    ar2src[...] = jnp.sum(arcv[...], axis=0)
-    for dx, dc in across:
-        send(ar2src, arcv2.at[x * 2 + c], 7, xpeer(dx, dc), 8)
-    arcv2[x * 2 + c] = ar2src[...]
 
     arrived(other_rows(db, dmargin, c), 9)
     build_windows(db, (1 - c) * (ROWS + dmargin), dmargin, dmargin, dwindows, 7)
-    banded(dwindows, dbands, 2, 0, (DK + 1) // 4, total)
+    banded(dwindows, dbands, 4, 0, (DK + 1) // 8, total)
 
     def unpair_filtered(q, carry):
         at = pl.ds(pl.multiple_of(q * CAP, CAP), CAP)
@@ -478,51 +499,53 @@
         tf[2 * q + 1] = total[at, PW:2 * PW]
         return carry
 
-    lax.fori_loop(0, ROWS // 2, unpair_filtered, 0, unroll=2)
+    lax.fori_loop(0, ROWS // 2, unpair_filtered, 0, unroll=6)
     for q in range(CAP):
         pltpu.make_async_copy(tf.at[:, q, :], significance.at[:, pl.ds(q * PW, PW)], local.at[3]).start()
-    arrived(arcv2.at[pl.ds(0, 7)], 8)
-    sums = jnp.sum(arcv2[...], axis=0)
+    arrived(arcv.at[pl.ds(0, GROUP - 1)], 8)
+    sums = jnp.sum(arcv[...], axis=0)
     whole_square = jnp.sum(jnp.where(lane1 == 0, sums, 0.0), axis=1, keepdims=True)
     whole_count = jnp.sum(jnp.where(lane1 == 1, sums, 0.0), axis=1, keepdims=True)
     level = whole_square / whole_count
     taps = detection_kernel[...].astype(F32)
     norm = jnp.sum(jnp.sum(taps * taps, axis=1, keepdims=True), axis=0, keepdims=True)
-    noise[...] = jnp.broadcast_to(level, (1, PW))
-    scale[...] = jnp.broadcast_to(1.0 / jnp.sqrt(1.0 + level * norm), (1, PW))
+    second = lax.broadcasted_iota(I32, (8, PW), 0) == 1
+    numbers[...] = jnp.where(second, 1.0 / jnp.sqrt(1.0 + level * norm), level)
+    report = pltpu.make_async_copy(numbers, stats, local.at[4])
+    report.start()
     sent(grcv.at[pl.ds(0, GROUP - 1)], 5)
-    sent(arcv.at[pl.ds(0, GROUP - 1)], 6)
-    sent(arcv2.at[pl.ds(0, 7)], 7)
+    sent(arcv2.at[pl.ds(0, 7)], 6)
+    sent(arcv.at[pl.ds(0, GROUP - 1)], 7)
     sent(db.at[pl.ds(0, dmargin)], 8)
     pltpu.make_async_copy(diffs, diffs, local.at[2]).wait()
     pltpu.make_async_copy(tf, tf, local.at[3]).wait()
+    report.wait()
 
 
 def other_rows(ref, margin, c):
     return ref.at[pl.ds((1 - c) * (ROWS + margin), margin)]
 
 
-def finish_kernel(difference, filtered, level, scale, out_difference, out_significance, noise, held, sums, factor, total, ins, outs):
-    parts = [slice(r, r + 8) for r in range(0, ROWS, 8)]
-    loads = [pltpu.make_async_copy(scale, factor, ins.at[0])]
-    loads += [pltpu.make_async_copy(filtered.at[at], sums.at[at], ins.at[1 + i]) for i, at in enumerate(parts)]
-    loads += [pltpu.make_async_copy(difference.at[at], held.at[at], ins.at[4 + i]) for i, at in enumerate(parts)]
-    loads += [pltpu.make_async_copy(level, total, ins.at[7])]
+def finish_kernel(difference, filtered, stats, out_difference, out_significance, out_noise, held, sums, numbers, ins, outs):
+    loads = [
+        pltpu.make_async_copy(stats, numbers, ins.at[0]),
+        pltpu.make_async_copy(filtered, sums, ins.at[1]),
+        pltpu.make_async_copy(difference, held, ins.at[2]),
+    ]
+    stores = [
+        pltpu.make_async_copy(numbers.at[pl.ds(0, 1)], out_noise, outs.at[0]),
+        pltpu.make_async_copy(sums, out_significance, outs.at[1]),
+        pltpu.make_async_copy(held, out_difference, outs.at[2]),
+    ]
     for load in loads:
         load.start()
     loads[0].wait()
-    stores = []
-    for i, at in enumerate(parts):
-        loads[1 + i].wait()
-        sums[at] = sums[at] * factor[0:1, 0:1]
-        stores.append(pltpu.make_async_copy(sums.at[at], out_significance.at[at], outs.at[i]))
-        stores[-1].start()
-    for i, at in enumerate(parts):
-        loads[4 + i].wait()
-        stores.append(pltpu.make_async_copy(held.at[at], out_difference.at[at], outs.at[3 + i]))
-        stores[-1].start()
-    loads[7].wait()
-    noise[...] = total[...]
+    stores[0].start()
+    loads[1].wait()
+    sums[...] = sums[...] * numbers[1:2, 0:1]
+    stores[1].start()
+    loads[2].wait()
+    stores[2].start()
     for store in stores:
         store.wait()
 
@@ -535,16 +558,15 @@
     far = pl.BlockSpec(memory_space=pl.ANY)
     wide = template.shape[2]
     margin, dmargin = KS // 2, DK // 2
-    difference, filtered, noise, scale = pl.pallas_call(
+    difference, filtered, stats = pl.pallas_call(
         kernel,
         out_shape=(
             jax.ShapeDtypeStruct((ROWS, wide), F32),
             jax.ShapeDtypeStruct((ROWS, wide), F32),
-            jax.ShapeDtypeStruct((1, PW), F32),
-            jax.ShapeDtypeStruct((1, PW), F32),
+            jax.ShapeDtypeStruct((8, PW), F32),
         ),
-        in_specs=[far] * 11,
-        out_specs=(far, far, vmem, vmem),
+        in_specs=[far, far, vmem, vmem] + [far] * 7,
+        out_specs=(far, far, far),
         scratch_shapes=[
             pltpu.VMEM((ROWS + HALO, NP, PW), F32),
             pltpu.VMEM((HALO, NP, PW), F32),
@@ -562,10 +584,11 @@
             pltpu.VMEM((NY * CAP, PW), F32),
             pltpu.VMEM((GROUP, ROWS, PW), BF16),
             pltpu.VMEM((GROUP, ROWS, PW), BF16),
+            pltpu.VMEM((GROUP, ROWS, PW), F32),
             pltpu.VMEM((48 * 8, PW), F32),
             pltpu.VMEM((48 * 8, PW), F32),
-            pltpu.VMEM(((KS + 1) * 2 * PW, 2 * PW), BF16),
-            pltpu.VMEM(((DK + 1) * 2 * PW, 2 * PW), BF16),
+            pltpu.VMEM(((KS + 2) * 2 * PW, PW), BF16),
+            pltpu.VMEM(((DK + 2) * 2 * PW, PW), BF16),
             pltpu.VMEM((2, (ROWS // 2 + margin) * CAP, 2 * PW), BF16),
             pltpu.VMEM((2, (ROWS // 2 + dmargin) * CAP, 2 * PW), BF16),
             pltpu.VMEM((ROWS // 2 * CAP, 2 * PW), F32),
@@ -576,11 +599,10 @@
             pltpu.VMEM((GROUP, 1, PW), F32),
             pltpu.VMEM((1, PW), F32),
             pltpu.VMEM((8, 1, PW), F32),
+            pltpu.VMEM((8, PW), F32),
             pltpu.SemaphoreType.DMA((13,)),
             pltpu.SemaphoreType.DMA((9,)),
-            pltpu.SemaphoreType.DMA((13,)),
-            pltpu.SMEM((1,), I32),
-            pltpu.SMEM((1,), I32),
+            pltpu.SemaphoreType.DMA((17,)),
             pltpu.VMEM((1, ROWS), BF16),
             pltpu.VMEM((1, NP * PW), BF16),
             pltpu.VMEM((1, NP), I32),
@@ -602,19 +624,18 @@
             jax.ShapeDtypeStruct((ROWS, wide), F32),
             jax.ShapeDtypeStruct((1, PW), F32),
         ),
-        in_specs=[far] * 4,
-        out_specs=(far, far, vmem),
+        in_specs=[far] * 3,
+        out_specs=(far, far, far),
         scratch_shapes=[
             pltpu.VMEM((ROWS, wide), F32),
             pltpu.VMEM((ROWS, wide), F32),
-            pltpu.VMEM((1, PW), F32),
-            pltpu.VMEM((1, PW), F32),
-            pltpu.SemaphoreType.DMA((8,)),
-            pltpu.SemaphoreType.DMA((6,)),
+            pltpu.VMEM((8, PW), F32),
+            pltpu.SemaphoreType.DMA((3,)),
+            pltpu.SemaphoreType.DMA((3,)),
         ],
         compiler_params=pltpu.CompilerParams(vmem_limit_bytes=60 * 1024 * 1024),
         name="finish",
-    )(difference, filtered, noise, scale)
+    )(difference, filtered, stats)
     return difference[None], significance[None], noise[0, 0]
 
 

time: 45.6 us -> 42.4 us (0.930)
  Pallas kernels: 43.5 us -> 40.2 us
    pallas_call x1, Pallas kernels: 40.9 us -> 38.2 us  [on_device(): pl.pallas_call(kernel, out_shape=(jax.ShapeDtypeStruct((ROWS, wide), F32)...]
    pallas_call x1, Pallas kernels: 2.56 us -> 1.99 us  [on_device(): pl.pallas_call(finish_kernel, out_shape=(jax.ShapeDtypeStruct((ROWS, wide...]
where the time goes in v3:
time: 42.4 us; the launch traced here: 42.2 us
  Pallas kernels  40.2 us (95%)
  between operations  1.93 us (5%)
    pallas_call x1, Pallas kernels, on_device(): pl.pallas_call(kernel, out_shape=(jax.ShapeDtypeStruct((ROWS, wide), F32)...  38.2 us
    pallas_call x1, Pallas kernels, on_device(): pl.pallas_call(finish_kernel, out_shape=(jax.ShapeDtypeStruct((ROWS, wide...  1.99 us

profile of v3, /device:TPU:1, one launch (start us, length us, event | category | flops | bytes accessed | tf_op | source)
XLA Modules:
  0.0 42.2 jit_solution(15519911317372633218)
XLA Ops:
  1.9 38.2 %warp_match_detect.1 = (f32[24,4096]{1,0:T(8,128)}, f32[24,4096]{1,0:T(8,128)}, f32[8,128]{1,0:T(8,128)}) custom-call(f32[24,2048]{1,0:T(8,128)} %bitcast.9, f32[24,4096]{1,0:T(8,128)} %bitcast.8, s32[1]{0:T(128)S(6)} %copy.14.rest_0_, s32[1]{0:T(128)S(6)} %copy.15.rest_1_, bf16[1,24]{1,0:T(2,128)(2,1)} %rest_2_.1, bf16[1,2048]{1,0:T(2,128)(2,1)} %rest_3_.1, ...), custom_call_target="tpu_custom_call" | custom-call | tf_op jit(solution)/shard_map/warp_match_detect/pallas_call | solution.py:561
  40.2 2.0 %finish.1 = (f32[24,4096]{1,0:T(8,128)}, f32[24,4096]{1,0:T(8,128)}, f32[1,128]{1,0:T(1,128)}) custom-call(f32[24,4096]{1,0:T(8,128)} %get-tuple-element.9.difference, f32[24,4096]{1,0:T(8,128)} %get-tuple-element.10.filtered, f32[8,128]{1,0:T(8,128)} %get-tuple-element.11.stats), custom_call_target="tpu_custom_call" | custom-call | tf_op jit(solution)/shard_map/finish/pallas_call | solution.py:620

commit v4 on v3

--- a/solution.py
+++ b/solution.py
@@ -106,9 +106,8 @@
     lax.fori_loop(0, count, step, 0)
 
 
-def near_first(i):
-    half = (i + 1) // 2
-    return lax.rem(half * (2 * (i % 2) - 1) + NZ, NZ)
+def rows_of(pz):
+    return pz * 3 % NZ if isinstance(pz, int) else lax.rem(pz * 3, NZ)
 
 
 def far_first(i):
@@ -225,10 +224,10 @@
     inside = lane16.astype(F32) < width16
     head = meta[...]
 
-    def fragments(pz):
+    def fragments(group):
         rows = []
         for j in range(FR):
-            r = pz * FR + j
+            r = group * FR + j
             w = rfw[r]
             mixed = ((1.0 - w) * ext[r + t] + w * ext[r + t + 1]).astype(BF16).astype(F32)
             leftward = pltpu.roll(mixed, left_turn, 1)
@@ -248,7 +247,7 @@
         return out
 
     def place_fragments(pz):
-        for py, value in enumerate(fragments(pz)):
+        for py, value in enumerate(fragments(rows_of(pz))):
             msg[pz * NY + py] = value
 
     def spread(pz):
@@ -266,13 +265,14 @@
             else:
                 pl.when(z != pz)(go)
 
-    for pz in range(EARLY):
+    planes = [rows_of(group) for group in range(NZ)]
+    for pz in planes[:EARLY]:
         place_fragments(pz)
     pl.semaphore_wait(barrier, len(near) + len(across))
 
     send(ext.at[pl.ds(0, HALO)], hx, 0, partner)
     send(tb.at[pl.ds(margin + (1 - c) * (ROWS - margin), margin)], tb.at[pl.ds(c * (ROWS + margin), margin)], 1, partner)
-    for pz in range(EARLY):
+    for pz in planes[:EARLY]:
         spread(pz)
     build_windows(tb, margin, ROWS, margin, windows, 4)
     arrived(hx, 0)
@@ -280,7 +280,7 @@
     for r in range(HALO):
         ext[ROWS + r] = hx[r] * keep
 
-    for pz in range(EARLY, NZ):
+    for pz in planes[EARLY:]:
         place_fragments(pz)
         spread(pz)
     rcv[me] = msg[me]
@@ -308,11 +308,8 @@
 
     arrived(other_rows(tb, margin, c), 1)
     build_windows(tb, (1 - c) * (ROWS + margin), margin, margin, windows, 4)
-    banded(windows, bands, 3, 0, 4, total)
+    banded(windows, bands, 3, 0, 7, total)
     forward(2, (0, 1, 7), 11)
-    banded(windows, bands, 3, 4, 7, total)
-    forward(3, (2, 6), 8)
-    forward(4, (3, 5, 4), 12)
 
     def unpair(q, carry):
         at = pl.ds(pl.multiple_of(q * CAP, CAP), CAP)
@@ -328,7 +325,7 @@
             value, last = None, []
             for j in range(FR):
                 turn = (FL * (j - py)) % PW
-                row = matched[pz * FR + j]
+                row = matched[rows_of(pz) * FR + j]
                 moved = pltpu.roll(row[:ROWS], turn, 1) if turn else row[:ROWS]
                 value = moved if value is None else jnp.where(lane24 >= FL * j, moved, value)
                 turn = (FL * (FR - py)) % PW
@@ -351,6 +348,8 @@
         _, py, device = zpeer(0, dy)
         send(mfr.at[z * NY + py], mrc.at[me], 4, device, 5)
     mrc[me] = mfr[me]
+    forward(3, (2, 6), 8)
+    forward(4, (3, 5, 4), 12)
 
     def codes(block):
         picks = (lanes_of((8, PW)) == lax.broadcasted_iota(I32, (8, PW), 0) + 96).astype(F32).astype(BF16)
@@ -477,7 +476,7 @@
                 rest = pltpu.roll(rest, turn, 1) if turn else rest
                 moved = jnp.concatenate([moved, rest], axis=0)
                 science = moved if science is None else jnp.where(lane32 >= FL * py, moved, science)
-            r = pz * FR + j
+            r = rows_of(pz) * FR + j
             value = jnp.where(live, science - matched[r], 0.0)
             diffs[r] = value
             db[dmargin + r] = value.astype(BF16)

time: 42.4 us -> 41.4 us (0.976)
  Pallas kernels: 40.2 us -> 39.3 us
    pallas_call x1, Pallas kernels: 38.2 us -> 37.3 us  [on_device(): pl.pallas_call(kernel, out_shape=(jax.ShapeDtypeStruct((ROWS, wide), F32)...]
where the time goes in v4:
time: 41.4 us; the launch traced here: 41.2 us
  Pallas kernels  39.3 us (95%)
  between operations  1.93 us (5%)
    pallas_call x1, Pallas kernels, on_device(): pl.pallas_call(kernel, out_shape=(jax.ShapeDtypeStruct((ROWS, wide), F32)...  37.3 us
    pallas_call x1, Pallas kernels, on_device(): pl.pallas_call(finish_kernel, out_shape=(jax.ShapeDtypeStruct((ROWS, wide...  1.99 us

profile of v4, /device:TPU:1, one launch (start us, length us, event | category | flops | bytes accessed | tf_op | source)
XLA Modules:
  0.0 41.2 jit_solution(7119011070823211595)
XLA Ops:
  1.9 37.3 %warp_match_detect.1 = (f32[24,4096]{1,0:T(8,128)}, f32[24,4096]{1,0:T(8,128)}, f32[8,128]{1,0:T(8,128)}) custom-call(f32[24,2048]{1,0:T(8,128)} %bitcast.9, f32[24,4096]{1,0:T(8,128)} %bitcast.8, s32[1]{0:T(128)S(6)} %copy.14.rest_0_, s32[1]{0:T(128)S(6)} %copy.15.rest_1_, bf16[1,24]{1,0:T(2,128)(2,1)} %rest_2_.1, bf16[1,2048]{1,0:T(2,128)(2,1)} %rest_3_.1, ...), custom_call_target="tpu_custom_call" | custom-call | tf_op jit(solution)/shard_map/warp_match_detect/pallas_call | solution.py:560
  39.2 2.0 %finish.1 = (f32[24,4096]{1,0:T(8,128)}, f32[24,4096]{1,0:T(8,128)}, f32[1,128]{1,0:T(1,128)}) custom-call(f32[24,4096]{1,0:T(8,128)} %get-tuple-element.9.difference, f32[24,4096]{1,0:T(8,128)} %get-tuple-element.10.filtered, f32[8,128]{1,0:T(8,128)} %get-tuple-element.11.stats), custom_call_target="tpu_custom_call" | custom-call | tf_op jit(solution)/shard_map/finish/pallas_call | solution.py:619

commit v5 on v4

--- a/solution.py
+++ b/solution.py
@@ -265,20 +265,25 @@
             else:
                 pl.when(z != pz)(go)
 
+    for r in range(HALO):
+        ext[ROWS + r] = jnp.zeros((NP, PW), F32)
     planes = [rows_of(group) for group in range(NZ)]
     for pz in planes[:EARLY]:
         place_fragments(pz)
     pl.semaphore_wait(barrier, len(near) + len(across))
 
-    send(ext.at[pl.ds(0, HALO)], hx, 0, partner)
+    pl.when(c == 1)(lambda: send(ext.at[pl.ds(0, HALO)], hx, 0, partner))
     send(tb.at[pl.ds(margin + (1 - c) * (ROWS - margin), margin)], tb.at[pl.ds(c * (ROWS + margin), margin)], 1, partner)
     for pz in planes[:EARLY]:
         spread(pz)
     build_windows(tb, margin, ROWS, margin, windows, 4)
-    arrived(hx, 0)
-    keep = jnp.where(c == 0, 1.0, 0.0)
-    for r in range(HALO):
-        ext[ROWS + r] = hx[r] * keep
+
+    @pl.when(c == 0)
+    def _():
+        arrived(hx, 0)
+        for r in range(HALO):
+            ext[ROWS + r] = hx[r]
+
 
     for pz in planes[EARLY:]:
         place_fragments(pz)
@@ -308,8 +313,11 @@
 
     arrived(other_rows(tb, margin, c), 1)
     build_windows(tb, (1 - c) * (ROWS + margin), margin, margin, windows, 4)
-    banded(windows, bands, 3, 0, 7, total)
+    banded(windows, bands, 3, 0, 5, total)
     forward(2, (0, 1, 7), 11)
+    forward(3, (2, 6), 8)
+    banded(windows, bands, 3, 5, 7, total)
+    forward(4, (3, 5, 4), 12)
 
     def unpair(q, carry):
         at = pl.ds(pl.multiple_of(q * CAP, CAP), CAP)
@@ -348,8 +356,6 @@
         _, py, device = zpeer(0, dy)
         send(mfr.at[z * NY + py], mrc.at[me], 4, device, 5)
     mrc[me] = mfr[me]
-    forward(3, (2, 6), 8)
-    forward(4, (3, 5, 4), 12)
 
     def codes(block):
         picks = (lanes_of((8, PW)) == lax.broadcasted_iota(I32, (8, PW), 0) + 96).astype(F32).astype(BF16)
@@ -454,7 +460,7 @@
     build_bands(base_lo, base_hi, dbands, DK, 5)
     sent(rcv.at[pl.ds(0, GROUP - 1)], 2)
     sent(agb, 3)
-    sent(hx, 0)
+    pl.when(c == 1)(lambda: sent(hx, 0))
     sent(tb.at[pl.ds(0, margin)], 1)
     sent(mrc.at[pl.ds(0, GROUP - 1)], 4)
     arrived(arcv2.at[pl.ds(0, 7)], 7)

time: 41.4 us -> 40.8 us (0.986)
  Pallas kernels: 39.3 us -> 38.7 us
    pallas_call x1, Pallas kernels: 37.3 us -> 36.7 us  [on_device(): pl.pallas_call(kernel, out_shape=(jax.ShapeDtypeStruct((ROWS, wide), F32)...]
where the time goes in v5:
time: 40.8 us; the launch traced here: 40.6 us
  Pallas kernels  38.7 us (95%)
  between operations  1.93 us (5%)
    pallas_call x1, Pallas kernels, on_device(): pl.pallas_call(kernel, out_shape=(jax.ShapeDtypeStruct((ROWS, wide), F32)...  36.7 us
    pallas_call x1, Pallas kernels, on_device(): pl.pallas_call(finish_kernel, out_shape=(jax.ShapeDtypeStruct((ROWS, wide...  1.99 us

profile of v5, /device:TPU:1, one launch (start us, length us, event | category | flops | bytes accessed | tf_op | source)
XLA Modules:
  0.0 40.6 jit_solution(10466887818493440430)
XLA Ops:
  1.9 36.7 %warp_match_detect.1 = (f32[24,4096]{1,0:T(8,128)}, f32[24,4096]{1,0:T(8,128)}, f32[8,128]{1,0:T(8,128)}) custom-call(f32[24,2048]{1,0:T(8,128)} %bitcast.9, f32[24,4096]{1,0:T(8,128)} %bitcast.8, s32[1]{0:T(128)S(6)} %copy.14.rest_0_, s32[1]{0:T(128)S(6)} %copy.15.rest_1_, bf16[1,24]{1,0:T(2,128)(2,1)} %rest_2_.1, bf16[1,2048]{1,0:T(2,128)(2,1)} %rest_3_.1, ...), custom_call_target="tpu_custom_call" | custom-call | tf_op jit(solution)/shard_map/warp_match_detect/pallas_call | solution.py:566
  38.6 2.0 %finish.1 = (f32[24,4096]{1,0:T(8,128)}, f32[24,4096]{1,0:T(8,128)}, f32[1,128]{1,0:T(1,128)}) custom-call(f32[24,4096]{1,0:T(8,128)} %get-tuple-element.9.difference, f32[24,4096]{1,0:T(8,128)} %get-tuple-element.10.filtered, f32[8,128]{1,0:T(8,128)} %get-tuple-element.11.stats), custom_call_target="tpu_custom_call" | custom-call | tf_op jit(solution)/shard_map/finish/pallas_call | solution.py:625

commit v6 on v5

--- a/solution.py
+++ b/solution.py
@@ -434,15 +434,19 @@
     live_count = ROWS * jnp.sum(width32, axis=0, keepdims=True)
     place = (lax.rem(lane24, FL) + FL * y).astype(F32)
 
-    def mark_live(k, carry):
-        value = acc[pl.ds(pl.multiple_of(k * CAP, CAP), CAP), :]
-        width = jnp.sum(jnp.where(lane32 == 98, value, 0.0), axis=1, keepdims=True)
-        last = jnp.concatenate([width[ROWS:]] * FR, axis=0)
-        width = jnp.where(lane24 < FR * FL, width[:ROWS], last)
-        alive[k] = jnp.where(place < width, 1.0, 0.0)
-        return carry
-
-    lax.fori_loop(0, GROUP, mark_live, 0, unroll=8)
+    spot = (lax.broadcasted_iota(I32, (PW, PW), 0) == 98).astype(F32).astype(BF16)
+
+    def mark_live(pz, carry):
+        value = acc[pl.ds(pl.multiple_of(pz * chunk, chunk), chunk), :].astype(BF16)
+        wide = jnp.dot(value, spot, preferred_element_type=F32)
+        for py in range(NY):
+            width = wide[py * CAP:(py + 1) * CAP]
+            last = jnp.concatenate([width[ROWS:]] * FR, axis=0)
+            width = jnp.where(lane24 < FR * FL, width[:ROWS], last)
+            alive[pz * NY + py] = jnp.where(place < width, 1.0, 0.0)
+        return carry
+
+    lax.fori_loop(0, NZ, mark_live, 0, unroll=4)
     arrived(mrc.at[pl.ds(0, GROUP - 1)], 5)
 
     def square(k, squares):

time: 40.8 us -> 40.3 us (0.988)
  Pallas kernels: 38.7 us -> 38.2 us
    pallas_call x1, Pallas kernels: 36.7 us -> 36.2 us  [on_device(): pl.pallas_call(kernel, out_shape=(jax.ShapeDtypeStruct((ROWS, wide), F32)...]
where the time goes in v6:
time: 40.3 us; the launch traced here: 40.2 us
  Pallas kernels  38.2 us (95%)
  between operations  1.93 us (5%)
    pallas_call x1, Pallas kernels, on_device(): pl.pallas_call(kernel, out_shape=(jax.ShapeDtypeStruct((ROWS, wide), F32)...  36.2 us
    pallas_call x1, Pallas kernels, on_device(): pl.pallas_call(finish_kernel, out_shape=(jax.ShapeDtypeStruct((ROWS, wide...  1.99 us

profile of v6, /device:TPU:1, one launch (start us, length us, event | category | flops | bytes accessed | tf_op | source)
XLA Modules:
  0.0 40.2 jit_solution(13844827113606996758)
XLA Ops:
  1.9 36.2 %warp_match_detect.1 = (f32[24,4096]{1,0:T(8,128)}, f32[24,4096]{1,0:T(8,128)}, f32[8,128]{1,0:T(8,128)}) custom-call(f32[24,2048]{1,0:T(8,128)} %bitcast.9, f32[24,4096]{1,0:T(8,128)} %bitcast.8, s32[1]{0:T(128)S(6)} %copy.14.rest_0_, s32[1]{0:T(128)S(6)} %copy.15.rest_1_, bf16[1,24]{1,0:T(2,128)(2,1)} %rest_2_.1, bf16[1,2048]{1,0:T(2,128)(2,1)} %rest_3_.1, ...), custom_call_target="tpu_custom_call" | custom-call | tf_op jit(solution)/shard_map/warp_match_detect/pallas_call | solution.py:570
  38.2 2.0 %finish.1 = (f32[24,4096]{1,0:T(8,128)}, f32[24,4096]{1,0:T(8,128)}, f32[1,128]{1,0:T(1,128)}) custom-call(f32[24,4096]{1,0:T(8,128)} %get-tuple-element.9.difference, f32[24,4096]{1,0:T(8,128)} %get-tuple-element.10.filtered, f32[8,128]{1,0:T(8,128)} %get-tuple-element.11.stats), custom_call_target="tpu_custom_call" | custom-call | tf_op jit(solution)/shard_map/finish/pallas_call | solution.py:629
